TPU v7x, 16 devices: a 4x2x1 block of a 4x4x8 slice. The times are simulated.
16 devices in a mesh: dp: 2 (over y, z), tp: 8 (over x, core).
Axes of the slice: x: 4, y: 2, z: 1, core: 2. Of those that a mesh axis runs over, the one named last changes fastest.
The devices are a block of a 4x4x8 slice.
Arguments:
- x_in: bfloat16 [32, 512, 3072], P('dp'), parts along dimension 0
- adapter_ids: int32 [32], P('dp'), parts along dimension 0
- gain_attn: float32 [3072], replicated
- gain_mlp: float32 [3072], replicated
- w_q: bfloat16 [3072, 32, 96], P(None, 'tp')
- w_k: bfloat16 [3072, 32, 96], P(None, 'tp')
- w_v: bfloat16 [3072, 32, 96], P(None, 'tp')
- w_o: bfloat16 [32, 96, 3072], P('tp')
- w_gate: bfloat16 [3072, 8192], P(None, 'tp')
- w_up: bfloat16 [3072, 8192], P(None, 'tp')
- w_down: bfloat16 [8192, 3072], P('tp')
- a_q: bfloat16 [16, 3072, 32], P(None, None, 'tp')
- b_q: bfloat16 [16, 32, 32, 96], P(None, None, 'tp')
- a_k: bfloat16 [16, 3072, 32], P(None, None, 'tp')
- b_k: bfloat16 [16, 32, 32, 96], P(None, None, 'tp')
- a_v: bfloat16 [16, 3072, 32], P(None, None, 'tp')
- b_v: bfloat16 [16, 32, 32, 96], P(None, None, 'tp')
- a_o: bfloat16 [16, 32, 96, 32], P(None, 'tp')
- b_o: bfloat16 [16, 32, 3072], P(None, None, 'tp')
- a_gate: bfloat16 [16, 3072, 32], P(None, None, 'tp')
- b_gate: bfloat16 [16, 32, 8192], P(None, None, 'tp')
- a_up: bfloat16 [16, 3072, 32], P(None, None, 'tp')
- b_up: bfloat16 [16, 32, 8192], P(None, None, 'tp')
- a_down: bfloat16 [16, 8192, 32], P(None, 'tp')
- b_down: bfloat16 [16, 32, 3072], P(None, None, 'tp')
Outputs:
- output: bfloat16 [32, 512, 3072], P('dp'), parts along dimension 0
There are 2 independent parts. A program takes and returns all parts, laid end to end along the dimension named above; an argument that names none is the same for every part.
All inputs are finite; a program needn't handle non-finite values.
Results may differ from a plain program's by a relative error of at most 0.02.
Values are sent between devices in bfloat16 or wider.
A program may use at most 768 MiB of HBM per device.

v0:
```python
import jax
import jax.numpy as jnp
from jax import lax
from jax.sharding import PartitionSpec as P

value_a10 = 16
RMS_EPS = 1e-5


def rms_scale(x_in, gain_vec):
    x_f32 = x_in.astype(jnp.float32)
    inv_rms = lax.rsqrt(jnp.mean(x_f32 * x_f32, axis=-1, keepdims=True) + RMS_EPS)
    return (x_f32 * inv_rms * gain_vec).astype(jnp.bfloat16)


def causal_attention(q_flat, k_flat, v_flat, kv_heads, head_dim):
    num_seqs, seq_len = q_flat.shape[0], q_flat.shape[1]
    q_group = q_flat.reshape(num_seqs, seq_len, kv_heads, -1, head_dim)
    k_group = k_flat.reshape(num_seqs, seq_len, kv_heads, head_dim)
    v_group = v_flat.reshape(num_seqs, seq_len, kv_heads, head_dim)
    scores = jnp.einsum('bqngd,bknd->bngqk', q_group, k_group, preferred_element_type=jnp.float32) * head_dim ** -0.5
    causal = jnp.arange(seq_len)[:, None] >= jnp.arange(seq_len)[None, :]
    prob_bf = jax.nn.softmax(jnp.where(causal, scores, -jnp.inf), axis=-1).astype(jnp.bfloat16)
    att_out = jnp.einsum('bngqk,bknd->bqngd', prob_bf, v_group, preferred_element_type=jnp.float32)
    return att_out.astype(jnp.bfloat16).reshape(num_seqs, seq_len, -1)


def column_proj(h_in, w_loc, a_sel, b_sel, scale):
    value_a9 = jnp.einsum('bsd,bdr->bsr', h_in, a_sel, preferred_element_type=jnp.float32).astype(jnp.bfloat16)
    value_a8 = lax.all_gather(value_a9, 'tp', axis=2, tiled=True)
    base_out = jnp.einsum('bsd,de->bse', h_in, w_loc, preferred_element_type=jnp.float32)
    array_b8 = jnp.einsum('bsr,bre->bse', value_a8, b_sel, preferred_element_type=jnp.float32)
    return (base_out + scale * array_b8).astype(jnp.bfloat16)


def row_proj(h_in, w_loc, a_sel, b_sel, scale, resid_full):
    base_part = jnp.einsum('bse,ed->bsd', h_in, w_loc, preferred_element_type=jnp.float32).astype(jnp.bfloat16)
    value_a9 = jnp.einsum('bse,ber->bsr', h_in, a_sel, preferred_element_type=jnp.float32).astype(jnp.bfloat16)
    base_sum = lax.psum_scatter(base_part, 'tp', scatter_dimension=2, tiled=True)
    value_a8 = lax.psum(value_a9, 'tp')
    width = base_sum.shape[2]
    resid_loc = lax.dynamic_slice_in_dim(resid_full, lax.axis_index('tp') * width, width, axis=2)
    array_b8 = jnp.einsum('bsr,brd->bsd', value_a8, b_sel, preferred_element_type=jnp.float32)
    out_loc = resid_loc.astype(jnp.float32) + base_sum.astype(jnp.float32) + scale * array_b8
    return lax.all_gather(out_loc.astype(jnp.bfloat16), 'tp', axis=2, tiled=True)


def solution(mesh):
    act_spec = P('dp', None, None)
    w_head_spec = P(None, 'tp', None)
    w_out_spec = P('tp', None, None)
    w_col_spec = P(None, 'tp')
    w_row_spec = P('tp', None)
    a_rank_spec = P(None, None, 'tp')
    b_head_spec = P(None, None, 'tp', None)
    b_col_spec = P(None, None, 'tp')
    a_head_spec = P(None, 'tp', None, None)
    a_row_spec = P(None, 'tp', None)
    in_specs = (act_spec, P('dp'), P(None), P(None), w_head_spec, w_head_spec, w_head_spec, w_out_spec,
                w_col_spec, w_col_spec, w_row_spec, a_rank_spec, b_head_spec, a_rank_spec, b_head_spec,
                a_rank_spec, b_head_spec, a_head_spec, b_col_spec, a_rank_spec, b_col_spec,
                a_rank_spec, b_col_spec, a_row_spec, b_col_spec)

    def local_layer(x_in, adapter_ids, gain_attn, gain_mlp, w_q, w_k, w_v, w_o, w_gate, w_up, w_down,
                    a_q, b_q, a_k, b_k, a_v, b_v, a_o, b_o, a_gate, b_gate, a_up, b_up, a_down, b_down):
        num_seqs, model_dim = x_in.shape[0], x_in.shape[2]
        rank = b_q.shape[1]
        scale = value_a10 / rank

        def per_sequence(stack):
            return jnp.take(stack, adapter_ids, axis=0)

        def column(h_in, w_loc, a_stack, b_stack):
            return column_proj(h_in, w_loc.reshape(model_dim, -1), per_sequence(a_stack),
                               per_sequence(b_stack).reshape(num_seqs, rank, -1), scale)

        h_norm = rms_scale(x_in, gain_attn)
        q_loc = column(h_norm, w_q, a_q, b_q)
        k_loc = column(h_norm, w_k, a_k, b_k)
        v_loc = column(h_norm, w_v, a_v, b_v)
        att_loc = causal_attention(q_loc, k_loc, v_loc, w_k.shape[1], w_k.shape[2])
        x_one = row_proj(att_loc, w_o.reshape(-1, model_dim), per_sequence(a_o).reshape(num_seqs, -1, rank),
                         per_sequence(b_o), scale, x_in)
        h_two = rms_scale(x_one, gain_mlp)
        gate_loc = column(h_two, w_gate, a_gate, b_gate)
        up_loc = column(h_two, w_up, a_up, b_up)
        mlp_mid = (jax.nn.silu(gate_loc.astype(jnp.float32)) * up_loc.astype(jnp.float32)).astype(jnp.bfloat16)
        return row_proj(mlp_mid, w_down, per_sequence(a_down), per_sequence(b_down), scale, x_one)

    return jax.shard_map(local_layer, mesh=mesh, in_specs=in_specs, out_specs=act_spec, check_vma=False)
```

profile of v0, /device:TPU:113, one launch (start us, length us, event | category | flops | bytes accessed | tf_op | source)
XLA Modules:
  0.0 1821.3 jit_solution(15820974235896058509)
XLA Ops:
  38.8 19.9 %convolution_convert_fusion.7 = bf16[16,512,4]{1,2,0:T(4,128)(2,1)S(1)} fusion(bf16[16,3072,4]{1,2,0:T(4,128)(2,1)S(1)} %gather_fusion.4, pred[16]{0:T(512)(128)(4,1)S(1)} %compare_and_fusion, bf16[16,512,3072]{2,1,0:T(8,128)(2,1)} %param.33, f32[3072]{0:T(1024)S(1)} %copy-done.27, f32[16,512]{1,0:T(8,128)S(1)} %add_rsqrt_fusion.1), kind=kOutput, calls=%fused_computation.58 | convolution fusion | flops 302219264 | bytes 50835472 | tf_op jit(solution)/shard_map/bsd,bdr->bsr/dot_general | solution.py:29
  58.7 19.8 %all_gather.22 = bf16[16,512,32]{1,0,2:T(8,128)(2,1)} all-gather(bf16[16,512,4]{1,0,2:T(8,128)(2,1)S(1)} %copy.50), channel_id=1, replica_groups=mesh['dp'=2,'tp'=8] {'tp'}, dimensions={2}, use_global_device_ids=true | all-gather | bytes 589824 | tf_op jit(solution)/shard_map/all_gather | solution.py:30
  81.7 19.9 %convolution_convert_fusion.6 = bf16[16,512,4]{1,2,0:T(4,128)(2,1)S(1)} fusion(bf16[16,3072,4]{1,2,0:T(4,128)(2,1)S(1)} %gather_fusion.6, pred[16]{0:T(512)(128)(4,1)S(1)} %compare_and_fusion, bf16[16,512,3072]{2,1,0:T(8,128)(2,1)} %param.33, f32[3072]{0:T(1024)S(1)} %copy-done.27, f32[16,512]{1,0:T(8,128)S(1)} %add_rsqrt_fusion.1), kind=kOutput, calls=%fused_computation.57 | convolution fusion | flops 302219264 | bytes 50835472 | tf_op jit(solution)/shard_map/bsd,bdr->bsr/dot_general | solution.py:29
  101.6 22.0 %all_gather.23 = bf16[16,512,32]{1,0,2:T(8,128)(2,1)} all-gather(bf16[16,512,4]{1,0,2:T(8,128)(2,1)S(1)} %copy.52), channel_id=1, replica_groups=mesh['dp'=2,'tp'=8] {'tp'}, dimensions={2}, use_global_device_ids=true | all-gather | bytes 589824 | tf_op jit(solution)/shard_map/all_gather | solution.py:30
  126.7 19.8 %convolution_convert_fusion.8 = bf16[16,512,4]{1,2,0:T(4,128)(2,1)S(1)} fusion(bf16[16,3072,4]{1,2,0:T(4,128)(2,1)S(1)} %gather_fusion.2, pred[16]{0:T(512)(128)(4,1)S(1)} %compare_and_fusion, bf16[16,512,3072]{2,1,0:T(8,128)(2,1)} %param.33, f32[3072]{0:T(1024)S(1)} %copy-done.27, f32[16,512]{1,0:T(8,128)S(1)} %add_rsqrt_fusion.1), kind=kOutput, calls=%fused_computation.59 | convolution fusion | flops 302219264 | bytes 50835472 | tf_op jit(solution)/shard_map/bsd,bdr->bsr/dot_general | solution.py:29
  146.6 22.8 %all_gather.21 = bf16[16,512,32]{1,0,2:T(8,128)(2,1)} all-gather(bf16[16,512,4]{1,0,2:T(8,128)(2,1)S(1)} %copy.48), channel_id=1, replica_groups=mesh['dp'=2,'tp'=8] {'tp'}, dimensions={2}, use_global_device_ids=true | all-gather | bytes 589824 | tf_op jit(solution)/shard_map/all_gather | solution.py:30
  180.3 29.7 %add_convert_fusion.5 = bf16[16,512,384]{1,2,0:T(8,128)(2,1)} fusion(f32[16,512,384]{1,2,0:T(8,128)} %fusion.35, bf16[3072,384,1]{0,1,2:T(8,128)(2,1)} %bitcast.76, bf16[16,512,3072]{2,1,0:T(8,128)(2,1)} %param.33, f32[3072]{0:T(1024)S(1)} %copy-done.27, f32[16,512]{1,0:T(8,128)S(1)} %add_rsqrt_fusion.1), kind=kOutput, calls=%fused_computation.46 | convolution fusion | flops 19437453312 | bytes 71610368 | tf_op jit(solution)/shard_map/bsd,de->bse/dot_general | solution.py:31
  216.6 29.3 %add_convert_fusion.4 = bf16[16,512,384]{1,2,0:T(8,128)(2,1)} fusion(f32[16,512,384]{1,2,0:T(8,128)} %fusion.33, bf16[3072,384,1]{0,1,2:T(8,128)(2,1)} %bitcast.77, bf16[16,512,3072]{2,1,0:T(8,128)(2,1)} %param.33, f32[3072]{0:T(1024)S(1)} %copy-done.27, f32[16,512]{1,0:T(8,128)S(1)} %add_rsqrt_fusion.1), kind=kOutput, calls=%fused_computation.45 | convolution fusion | flops 19437453312 | bytes 71610368 | tf_op jit(solution)/shard_map/bsd,de->bse/dot_general | solution.py:31
  245.9 28.8 %fusion.7 = (f32[16,4,512]{2,1,0:T(4,128)}, f32[16,4,512,512]{3,2,1,0:T(8,128)}) fusion(pred[512,512]{0,1:T(8,128)(4,1)S(1)} %copy-done.8, bf16[16,512,4,96]{1,3,2,0:T(8,128)(2,1)} %bitcast.72, bf16[16,512,4,96]{1,3,2,0:T(8,128)(2,1)} %bitcast.73), kind=kOutput, calls=%fused_computation.28 | convolution fusion | flops 3271524352 | bytes 80084992 | tf_op jit(solution)/shard_map/bqngd,bknd->bngqk/dot_general | solution.py:21
  274.7 22.4 %fusion.6 = f32[16,4,512]{2,1,0:T(4,128)} fusion(f32[16,4,512,512]{3,2,1,0:T(8,128)} %get-tuple-element.13, f32[16,4,512]{2,1,0:T(4,128)} %get-tuple-element.12, pred[512,512]{0,1:T(8,128)(4,1)S(1)} %copy-done.8), kind=kLoop, calls=%fused_computation.27 | loop fusion | flops 67076096 | bytes 67633152 | tf_op jit(solution)/shard_map/reduce_sum | solution.py:23
  303.8 29.4 %add_convert_fusion.6 = bf16[16,512,384]{1,2,0:T(8,128)(2,1)} fusion(f32[16,512,384]{1,2,0:T(8,128)} %fusion.37, bf16[3072,384,1]{0,1,2:T(8,128)(2,1)} %bitcast.78, bf16[16,512,3072]{2,1,0:T(8,128)(2,1)} %param.33, f32[3072]{0:T(1024)S(1)} %copy-done.27, f32[16,512]{1,0:T(8,128)} %copy-done.23), kind=kOutput, calls=%fused_computation.47 | convolution fusion | flops 19437453312 | bytes 71610368 | tf_op jit(solution)/shard_map/bsd,de->bse/dot_general | solution.py:31
  333.2 31.9 %fusion.20 = bf16[16,4,96,512]{3,2,1,0:T(8,128)(2,1)} fusion(bf16[16,512,4,96]{1,3,2,0:T(8,128)(2,1)} %bitcast.79, f32[16,4,512]{2,1,0:T(4,128)S(1)} %copy-done.22, f32[16,4,512]{2,1,0:T(4,128)S(1)} %copy-done.17, f32[16,4,512,512]{3,2,1,0:T(8,128)} %get-tuple-element.13, pred[512,512]{0,1:T(8,128)(4,1)S(1)} %copy-done.8), kind=kOutput, calls=%fused_computation.52 | convolution fusion | flops 3308257280 | bytes 80216064 | tf_op jit(solution)/shard_map/bngqk,bknd->bqngd/dot_general | solution.py:24
  370.1 35.1 %convolution_convert_fusion.1 = bf16[16,512,3072]{1,2,0:T(8,128)(2,1)} fusion(bf16[16,512,384]{1,2,0:T(8,128)(2,1)} %bitcast.75, bf16[384,3072,1]{1,0,2:T(8,128)(2,1)S(1)} %bitcast.71), kind=kOutput, calls=%fused_computation.42 | convolution fusion | flops 19352518656 | bytes 58982400 | tf_op jit(solution)/shard_map/bse,ed->bsd/dot_general | solution.py:37
  427.2 248.5 %reduce-scatter.3.cloned.1.call-done = bf16[16,512,384]{1,2,0:T(8,128)(2,1)} async-done(((bf16[16,512,3072]{1,2,0:T(8,128)(2,1)}), bf16[16,512,384]{1,2,0:T(8,128)(2,1)}) %reduce-scatter.3.cloned.1.call-update) | async-done | bytes 6291472 | tf_op jit(solution)/shard_map/reduce_scatter | solution.py:39
  694.1 216.2 %all-gather.3.cloned.1.call-done = bf16[16,512,3072]{1,2,0:T(8,128)(2,1)} async-done(((bf16[16,512,384]{1,2,0:T(8,128)(2,1)}), bf16[16,512,3072]{1,2,0:T(8,128)(2,1)}) %all-gather.3.cloned.1.call-update) | async-done | bytes 50331664 | tf_op jit(solution)/shard_map/all_gather | solution.py:45
  926.6 33.9 %fusion.5 = bf16[16,512,3072]{1,2,0:T(8,128)(2,1)} fusion(bf16[16,512,3072]{1,2,0:T(8,128)(2,1)} %all-gather.3.cloned.1.call-done, f32[3072]{0:T(1024)S(1)} %copy-done.26, f32[16,512]{1,0:T(8,128)S(1)} %add_rsqrt_fusion), kind=kLoop, calls=%fused_computation.23 | loop fusion | flops 100663296 | bytes 100708352 | tf_op jit(solution)/shard_map/convert_element_type | solution.py:13
  994.7 17.3 convolution_convert_fusion.5
  1012.0 22.3 %all_gather.25 = bf16[16,512,32]{1,0,2:T(8,128)(2,1)S(1)} all-gather(bf16[16,512,4]{1,0,2:T(8,128)(2,1)S(1)} %copy.62), channel_id=1, replica_groups=mesh['dp'=2,'tp'=8] {'tp'}, dimensions={2}, use_global_device_ids=true | all-gather | bytes 589824 | tf_op jit(solution)/shard_map/all_gather | solution.py:30
  1034.3 60.7 %fusion.18 = f32[16,512,1024]{2,1,0:T(8,128)} fusion(bf16[16,512,3072]{1,2,0:T(8,128)(2,1)} %fusion.5, bf16[3072,1024]{1,0:T(8,128)(2,1)} %param.41), kind=kOutput, calls=%fused_computation.50 | convolution fusion | flops 51539607552 | bytes 90177536 | tf_op jit(solution)/shard_map/bsd,de->bse/dot_general | solution.py:31
  1121.4 72.7 %fusion.14 = bf16[16,512,1024]{2,1,0:T(8,128)(2,1)} fusion(f32[16,512,1024]{2,1,0:T(8,128)} %fusion.18, f32[16,512,1024]{2,1,0:T(8,128)} %fusion.25, f32[16,512,1024]{2,1,0:T(8,128)} %fusion.23, bf16[16,512,3072]{1,2,0:T(8,128)(2,1)} %fusion.5, bf16[3072,1024]{1,0:T(8,128)(2,1)} %param.42), kind=kOutput, calls=%fused_computation.39 | convolution fusion | flops 51657048064 | bytes 174063616 | tf_op jit(solution)/shard_map/bsd,de->bse/dot_general | solution.py:31
  1203.6 60.7 %convolution_convert_fusion = bf16[16,512,3072]{1,2,0:T(8,128)(2,1)} fusion(bf16[16,512,1024]{2,1,0:T(8,128)(2,1)} %fusion.14, bf16[1024,3072]{1,0:T(8,128)(2,1)} %param.43), kind=kOutput, calls=%fused_computation.41 | convolution fusion | flops 51564773376 | bytes 73400320 | tf_op jit(solution)/shard_map/bse,ed->bsd/dot_general | solution.py:37
  1266.1 249.0 %reduce-scatter.5.cloned.1.call-done = bf16[16,512,384]{1,2,0:T(8,128)(2,1)} async-done(((bf16[16,512,3072]{1,2,0:T(8,128)(2,1)}), bf16[16,512,384]{1,2,0:T(8,128)(2,1)}) %reduce-scatter.5.cloned.1.call-update) | async-done | bytes 6291472 | tf_op jit(solution)/shard_map/reduce_scatter | solution.py:39
  1525.6 224.2 %all-gather.5.cloned.1.call-done = bf16[16,512,3072]{1,2,0:T(8,128)(2,1)} async-done(((bf16[16,512,384]{1,2,0:T(8,128)(2,1)}), bf16[16,512,3072]{1,2,0:T(8,128)(2,1)}) %all-gather.5.cloned.1.call-update) | async-done | bytes 50331664 | tf_op jit(solution)/shard_map/all_gather | solution.py:45
  1749.8 64.5 %copy.70 = bf16[16,512,3072]{2,1,0:T(8,128)(2,1)} copy(bf16[16,512,3072]{1,2,0:T(8,128)(2,1)} %all-gather.5.cloned.1.call-done) | data formatting | bytes 100663296 | tf_op jit(solution)/shard_map/all_gather | solution.py:45
  (116 shorter events, 206.4 us)
Async XLA Ops:
  6.5 363.6 %copy-start = (bf16[4,96,3072]{2,1,0:T(8,128)(2,1)S(1)}, bf16[4,96,3072]{2,1,0:T(8,128)(2,1)}, u32[]{:S(2)}) copy-start(bf16[4,96,3072]{2,1,0:T(8,128)(2,1)} %param.40) | copy-start | bytes 7077892
  6.6 420.6 %all-reduce.3.cloned.1.call-start = ((), (), s32[]{:S(2)}) async-start(), calls=%async_computation.3 | async-start | bytes 1048576 | tf_op jit(solution)/shard_map/psum | solution.py:40
  8.0 118.7 %copy-start.18 = (pred[16]{0:T(512)(128)(4,1)}, pred[16]{0:T(512)(128)(4,1)S(1)}, u32[]{:S(2)}) copy-start(pred[16]{0:T(512)(128)(4,1)S(1)} %compare_and_fusion) | copy-start | bytes 52
  8.8 160.5 %copy-start.24 = (s32[1024]{0:T(1024)}, s32[1024]{0:T(1024)S(1)}, u32[]{:S(2)}) copy-start(s32[1024]{0:T(1024)S(1)} %pad_clamp_fusion) | copy-start | bytes 12292
  38.8 177.8 %copy-start.23 = (f32[16,512]{1,0:T(8,128)}, f32[16,512]{1,0:T(8,128)S(1)}, u32[]{:S(2)}) copy-start(f32[16,512]{1,0:T(8,128)S(1)} %add_rsqrt_fusion.1) | copy-start | bytes 98308
  38.8 42.0 %copy-start.2 = (bf16[16,3072,4]{1,2,0:T(4,128)(2,1)S(1)}, bf16[16,3072,4]{1,2,0:T(4,128)(2,1)}, u32[]{:S(2)}) copy-start(bf16[16,3072,4]{1,2,0:T(4,128)(2,1)} %param.44) | copy-start | bytes 1179652
  81.7 44.1 %copy-start.3 = (bf16[16,3072,4]{1,2,0:T(4,128)(2,1)S(1)}, bf16[16,3072,4]{1,2,0:T(4,128)(2,1)}, u32[]{:S(2)}) copy-start(bf16[16,3072,4]{1,2,0:T(4,128)(2,1)} %param.48) | copy-start | bytes 1179652
  180.3 29.8 %copy-start.12 = (bf16[16,512,32]{1,0,2:T(8,128)(2,1)S(1)}, bf16[16,512,32]{1,0,2:T(8,128)(2,1)}, u32[]{:S(2)}) copy-start(bf16[16,512,32]{1,0,2:T(8,128)(2,1)} %all_gather.23) | copy-start | bytes 1572868
  180.3 29.8 %copy-start.15 = (bf16[16,32,384]{2,1,0:T(8,128)(2,1)S(1)}, bf16[16,32,384]{2,1,0:T(8,128)(2,1)}, u32[]{:S(2)}) copy-start(bf16[16,32,384]{2,1,0:T(8,128)(2,1)} %reshape.105) | copy-start | bytes 1179652
  303.8 29.4 %copy-start.22 = (f32[16,4,512]{2,1,0:T(4,128)S(1)}, f32[16,4,512]{2,1,0:T(4,128)}, u32[]{:S(2)}) copy-start(f32[16,4,512]{2,1,0:T(4,128)} %fusion.6) | copy-start | bytes 393220
  333.2 32.0 %copy-start.14 = (bf16[16,384,32]{1,2,0:T(8,128)(2,1)S(1)}, bf16[16,384,32]{1,2,0:T(8,128)(2,1)}, u32[]{:S(2)}) copy-start(bf16[16,384,32]{1,2,0:T(8,128)(2,1)} %gather.23) | copy-start | bytes 1179652
  333.2 31.9 %copy-start.19 = (pred[16]{0:T(512)(128)(4,1)S(1)}, pred[16]{0:T(512)(128)(4,1)}, u32[]{:S(2)}) copy-start(pred[16]{0:T(512)(128)(4,1)} %copy-done.18) | copy-start | bytes 52
  370.0 305.7 %reduce-scatter.3.cloned.1.call-start = ((), (), s32[]{:S(2)}) async-start(), calls=%async_computation.2 | async-start | bytes 56623104 | tf_op jit(solution)/shard_map/reduce_scatter | solution.py:39
  405.3 281.0 %copy-start.4 = (bf16[16,3072,4]{1,2,0:T(4,128)(2,1)S(1)}, bf16[16,3072,4]{1,2,0:T(4,128)(2,1)}, u32[]{:S(2)}) copy-start(bf16[16,3072,4]{1,2,0:T(4,128)(2,1)} %param.54) | copy-start | bytes 1179652
  405.3 505.0 %all-gather.3.cloned.1.call-start = ((), (), s32[]{:S(2)}) async-start(), calls=%async_computation.4 | async-start | bytes 56623104 | tf_op jit(solution)/shard_map/all_gather | solution.py:45
  413.1 274.1 %copy-start.16 = (bf16[16,32,1024]{2,1,0:T(8,128)(2,1)S(1)}, bf16[16,32,1024]{2,1,0:T(8,128)(2,1)}, u32[]{:S(2)}) copy-start(bf16[16,32,1024]{2,1,0:T(8,128)(2,1)} %param.55) | copy-start | bytes 3145732
  413.1 275.7 %copy-start.5 = (bf16[16,3072,4]{1,2,0:T(4,128)(2,1)S(1)}, bf16[16,3072,4]{1,2,0:T(4,128)(2,1)}, u32[]{:S(2)}) copy-start(bf16[16,3072,4]{1,2,0:T(4,128)(2,1)} %param.52) | copy-start | bytes 1179652
  686.1 580.0 %all-reduce.5.cloned.1.call-start = ((), (), s32[]{:S(2)}) async-start(), calls=%async_computation.6 | async-start | bytes 1048576 | tf_op jit(solution)/shard_map/psum | solution.py:40
  689.6 236.9 %copy-start.26 = (f32[3072]{0:T(1024)S(1)}, f32[3072]{0:T(1024)}, u32[]{:S(2)}) copy-start(f32[3072]{0:T(1024)} %param.36) | copy-start | bytes 36868
  1034.3 60.7 %copy-start.10 = (bf16[16,32,1024]{2,1,0:T(8,128)(2,1)S(1)}, bf16[16,32,1024]{2,1,0:T(8,128)(2,1)}, u32[]{:S(2)}) copy-start(bf16[16,32,1024]{2,1,0:T(8,128)(2,1)} %gather_fusion.12) | copy-start | bytes 3145732
  1121.4 72.7 %copy-start.7 = (bf16[16,1024,32]{1,2,0:T(8,128)(2,1)S(1)}, bf16[16,1024,32]{1,2,0:T(8,128)(2,1)}, u32[]{:S(2)}) copy-start(bf16[16,1024,32]{1,2,0:T(8,128)(2,1)} %gather_fusion.1) | copy-start | bytes 3145732
  1203.5 311.6 %reduce-scatter.5.cloned.1.call-start = ((), (), s32[]{:S(2)}) async-start(), calls=%async_computation.5 | async-start | bytes 56623104 | tf_op jit(solution)/shard_map/reduce_scatter | solution.py:39
  1264.4 485.4 %all-gather.5.cloned.1.call-start = ((), (), s32[]{:S(2)}) async-start(), calls=%async_computation.7 | async-start | bytes 56623104 | tf_op jit(solution)/shard_map/all_gather | solution.py:45
  1525.6 288.7 %copy-start.1 = (bf16[4,96,3072]{2,1,0:T(8,128)(2,1)S(1)}, bf16[4,96,3072]{2,1,0:T(8,128)(2,1)}, u32[]{:S(2)}) copy-start(bf16[4,96,3072]{2,1,0:T(8,128)(2,1)} %param.40) | copy-start | bytes 7077892
  (10 other events, 144.4 us)
Sparse Core Ops, SparseCore 0:
  370.1 56.9 all-reduce.2
  429.5 246.1 reduce-scatter.2
  686.3 223.9 all-gather.2
  1203.7 56.2 all-reduce.4
  1264.5 250.5 reduce-scatter.4
  1525.7 223.9 all-gather.4
where the time goes:
time: 1830 us; the launch traced here: 1820 us
  waiting for transfers between devices  944 us (52%)
  matrix products  555 us (30%)
  local copies, waits for them, and re-layouts  111 us (6%)
  blocking collectives  104 us (6%)
  other arithmetic  94.1 us (5%)
    reduce_scatter x2, waiting for transfers between devices, row_proj(): lax.psum_scatter(base_part, 'tp', scatter_dimension=2, tiled=True)  498 us
    all_gather x2, waiting for transfers between devices, row_proj(): lax.all_gather(out_loc.astype(jnp.bfloat16), 'tp', axis=2, tiled=True)  440 us
    dot_general x5, matrix products, column_proj(): jnp.einsum('bsd,de->bse', h_in, w_loc, preferred_element_type=jnp.float32)  222 us
    all_gather x5, blocking collectives, column_proj(): value_a8 = lax.all_gather(value_a9, 'tp', axis=2, tiled=True)  104 us
    dot_general x2, matrix products, row_proj(): jnp.einsum('bse,ed->bsd', h_in, w_loc, preferred_element_type=jnp.float32)  95.8 us
    dot_general x5, matrix products, column_proj(): jnp.einsum('bsd,bdr->bsr', h_in, a_sel, preferred_element_type=jnp.float32)  94.3 us
    all_gather x1, local copies, waits for them, and re-layouts, row_proj(): lax.all_gather(out_loc.astype(jnp.bfloat16), 'tp', axis=2, tiled=True)  64.5 us
    dot_general x5, matrix products, column_proj(): jnp.einsum('bsr,bre->bse', value_a8, b_sel, preferred_element_type=jnp.fl...  47.3 us
  transfers between devices with their start and end apart: 6, of which 5 were waited for; matrix products, arithmetic and copies ran while one was open for 7% of the time, Pallas kernels for 0%

commit v1 on v0

v1 whole, which is shorter than its diff:
```python
import functools
import math

import jax
import jax.numpy as jnp
from jax import lax
from jax.experimental import pallas as pl
from jax.experimental.pallas import tpu as pltpu
from jax.sharding import PartitionSpec as P

LORA_ALPHA = 16
RMS_EPS = 1e-5
CORES = 2
MESH = pl.DeviceIdType.MESH
F32, BF16 = jnp.float32, jnp.bfloat16
NT = (((1,), (1,)), ((), ()))
VMEM_LIMIT = 67_000_000


def dot(a, b):
    return jnp.dot(a, b, preferred_element_type=F32)


def dot_nt(a, b):
    return lax.dot_general(a, b, NT, preferred_element_type=F32)


def ring(n):
    me = lax.axis_index("tp")
    core, chip = lax.rem(me, CORES), lax.div(me, CORES)
    right = lax.rem(chip + 1, n) * CORES + core
    left = lax.rem(chip + n - 1, n) * CORES + core
    return core, chip, right, left, chip * CORES + 1 - core


def greet(*others):
    barrier = pltpu.get_barrier_semaphore()
    for other in others:
        pl.semaphore_signal(barrier, inc=1, device_id={"tp": other}, device_id_type=MESH)
    pl.semaphore_wait(barrier, len(others))


def remote(src, dst, send, recv, to):
    return pltpu.make_async_remote_copy(src_ref=src, dst_ref=dst, send_sem=send, recv_sem=recv, device_id={"tp": to},
                                        device_id_type=MESH)


def local(src, dst, sem):
    return pltpu.make_async_copy(src, dst, sem)


def rms_rows(src, dst, gain, rows, step):
    def chunk(k, carry):
        at = pl.ds(pl.multiple_of(k * step, step), step)
        v = src[at, :].astype(F32)
        inv = lax.rsqrt(jnp.mean(v * v, axis=-1, keepdims=True) + RMS_EPS)
        dst[at, :] = (v * inv * gain[...]).astype(BF16)
        return carry

    lax.fori_loop(0, rows // step, chunk, 0)


def head_windows(group, dim):
    out = []
    for h in range(group):
        lo, hi = h * dim, (h + 1) * dim
        start, stop = lo // 128 * 128, -(-hi // 128) * 128
        out.append((start, stop, lo - start, hi - start))
    return out


def attend(qkv, out, width, group, dim, qblock):
    seq = qkv.shape[0]
    lanes = group * dim

    def one_group(g, carry):
        base = pl.multiple_of(g * lanes, 128)
        for qb in range(seq // qblock):
            rows, keys = pl.ds(qb * qblock, qblock), (qb + 1) * qblock
            acc = [None] * (lanes // 128)
            mask = (lax.broadcasted_iota(jnp.int32, (qblock, keys), 0) + qb * qblock
                    >= lax.broadcasted_iota(jnp.int32, (qblock, keys), 1))
            for start, stop, lo, hi in head_windows(group, dim):
                size = stop - start
                lane_q = lax.broadcasted_iota(jnp.int32, (qblock, size), 1)
                lane_k = lax.broadcasted_iota(jnp.int32, (keys, size), 1)
                q = qkv[rows, pl.ds(base + start, size)]
                k = qkv[pl.ds(0, keys), pl.ds(width + base + start, size)]
                v = qkv[pl.ds(0, keys), pl.ds(2 * width + base + start, size)]
                q = jnp.where((lane_q >= lo) & (lane_q < hi), q, jnp.zeros_like(q))
                v = jnp.where((lane_k >= lo) & (lane_k < hi), v, jnp.zeros_like(v))
                scores = jnp.where(mask, dot_nt(q, k) * dim ** -0.5, -jnp.inf)
                top = jnp.max(scores, axis=-1, keepdims=True)
                e = jnp.exp(scores - top)
                prob = (e / jnp.sum(e, axis=-1, keepdims=True)).astype(BF16)
                o = dot(prob, v)
                for t in range(size // 128):
                    piece = o[:, t * 128:(t + 1) * 128]
                    j = start // 128 + t
                    acc[j] = piece if acc[j] is None else acc[j] + piece
            for j, piece in enumerate(acc):
                out[rows, pl.ds(base + j * 128, 128)] = piece.astype(BF16)
        return carry

    lax.fori_loop(0, width // lanes, one_group, 0)


def pick(shape, share, ranks, slots, axis):
    i = lax.broadcasted_iota(jnp.int32, shape, axis)
    t = lax.broadcasted_iota(jnp.int32, shape, 1 - axis)
    dev, slot, r = i // (slots * share), (i // share) % slots, i % share
    return jnp.where(t == slot * ranks + dev * share + r, 1.0, 0.0).astype(BF16)


def kernel_a(n, lag, keep, scale, group, dim, share,
             x, gain, wq, wk, wv, ar, bqkv, wide, agu, wo, wg, wu, wd, lml,
             att, ar_oth, b_oth, wide_f, agu_f, wo_f, wg_o, wu_o, wd_o, lml_o,
             wbuf, xbuf, hbuf, abuf, bbuf, qkv, attb, mids, sel,
             w_sem, x_sem, a_sem, bo_sem, bp_sem, d_send, d_recv, o_send, o_recv, m_send, m_recv,
             p_own, pr_send, pl_send, prl_recv, prr_recv, pfr_send, pfl_send, pfl_recv, pfr_recv, pp_send, pp_recv,
             r_send, l_send, own_sem, rl_recv, rr_recv, fr_send, fl_send, fl_recv, fr_recv):
    core, chip, right, left, partner = ring(n)
    before, after, opposite = lax.rem(chip + n - 1, n), lax.rem(chip + 1, n), lax.rem(chip + 2, n)
    across = opposite * CORES + core
    nseq, rows, own = x.shape[0] // CORES, x.shape[1], wq.shape[0]
    width = own * CORES
    first = core * nseq
    rank = bqkv.shape[1] // 3
    arows = ar.shape[1]
    crows = CORES * arows
    greet(right, left, partner, across)

    theirs, mine_at = pl.ds((1 - core) * nseq, nseq), pl.ds(first, nseq)
    near = [remote(ar.at[theirs], ar_oth, d_send.at[4], d_recv.at[4], partner)]
    near += [remote(w, wbuf.at[pl.ds(p * width + core * own, own)], d_send.at[p], d_recv.at[p], partner)
             for p, w in enumerate((wq, wk, wv))]
    near.append(remote(bqkv.at[theirs], b_oth, d_send.at[3], d_recv.at[3], partner))
    far = [remote(src, dst, o_send.at[k], o_recv.at[k], partner)
           for k, (src, dst) in enumerate(((lml.at[theirs], lml_o), (wg, wg_o), (wu, wu_o), (wd, wd_o)))]
    mine = [local(w, wbuf.at[pl.ds(p * width + core * own, own)], w_sem.at[p]) for p, w in enumerate((wq, wk, wv))]

    packs = [(wide, wide_f, True), (agu, agu_f, True), (wo, wo_f, False)]

    def pack_start(k):
        src, dst, _ = packs[k]
        remote(src, dst.at[chip, core], pr_send.at[k], prl_recv.at[k], right).start()
        remote(src, dst.at[chip, core], pl_send.at[k], prr_recv.at[k], left).start()
        local(src, dst.at[chip, core], p_own.at[k]).start()

    def pack_hops(k):
        src, dst, _ = packs[k]
        half = src.shape[0] // 2
        a, b = dst.at[before, core, pl.ds(0, half)], dst.at[after, core, pl.ds(half, half)]
        return remote(a, a, pfr_send.at[k], pfl_recv.at[k], right), remote(b, b, pfl_send.at[k], pfr_recv.at[k], left)

    def pack_pass(k):
        src, dst, _ = packs[k]
        hop_r, hop_l = pack_hops(k)
        remote(src, dst.at[before, core], pr_send.at[k], prl_recv.at[k], right).wait_recv()
        hop_r.start()
        remote(src, dst.at[after, core], pl_send.at[k], prr_recv.at[k], left).wait_recv()
        hop_l.start()

    def pack_push(k):
        src, dst, by_seq = packs[k]
        part = dst.at[:, core, theirs] if by_seq else dst.at[:, core]
        return remote(part, part, pp_send.at[k], pp_recv.at[k], partner)

    def pack_across(k):
        src, dst, _ = packs[k]
        half = src.shape[0] // 2
        local(src, dst.at[chip, core], p_own.at[k]).wait()
        a, b = dst.at[opposite, core, pl.ds(0, half)], dst.at[opposite, core, pl.ds(half, half)]
        remote(a, a, pfr_send.at[k], pfl_recv.at[k], right).wait_recv()
        remote(b, b, pfl_send.at[k], pfr_recv.at[k], left).wait_recv()
        pack_push(k).start()

    def pack_end(k):
        src, dst, by_seq = packs[k]
        remote(src, dst.at[chip, core], pr_send.at[k], prl_recv.at[k], right).wait_send()
        remote(src, dst.at[chip, core], pl_send.at[k], prr_recv.at[k], left).wait_send()
        for hop in pack_hops(k):
            hop.wait_send()
        pack_push(k).wait_send()
        part = dst.at[:, 1 - core, mine_at] if by_seq else dst.at[:, 1 - core]
        remote(part, part, pp_send.at[k], pp_recv.at[k], partner).wait_recv()

    def x_copy(g):
        return local(x.at[first + lax.rem(g, nseq)], xbuf.at[lax.rem(g, 2)], x_sem.at[lax.rem(g, 2)])

    def a_copies(s):
        slot = lax.rem(s, 2)
        own_at = pl.ds(pl.multiple_of(core * arows, arows), arows)
        oth_at = pl.ds(pl.multiple_of((1 - core) * arows, arows), arows)
        return [local(ar.at[first + s], abuf.at[slot, own_at], a_sem.at[slot, 0]),
                local(ar_oth.at[s], abuf.at[slot, oth_at], a_sem.at[slot, 1])]

    def b_copies(s):
        slot, out = lax.rem(s, 2), []
        for p in range(3):
            part = pl.ds(p * rank, rank)
            own_at = pl.ds(pl.multiple_of(core * own, 128), own)
            oth_at = pl.ds(pl.multiple_of((1 - core) * own, 128), own)
            out.append(local(bqkv.at[first + s, part], bbuf.at[slot, p, part, own_at], bo_sem.at[slot, p]))
            out.append(local(b_oth.at[s, part], bbuf.at[slot, p, part, oth_at], bp_sem.at[slot, p]))
        return out

    near[0].start()
    pack_start(0)
    for c in near[1:] + mine:
        c.start()
    x_copy(0).start()
    bbuf[...] = jnp.zeros_like(bbuf)
    sel[...] = pick(sel.shape, share, rank, arows // share, 1)
    near[0].wait()
    for c in a_copies(0):
        c.start()

    def rank_rows(j):
        return pl.ds(pl.multiple_of(j * crows, crows), crows)

    def mid_copies(s, source=None):
        froms = (chip, chip, chip) if source is None else source
        return [remote(mids.at[s, rank_rows(j)], mids.at[s, rank_rows(j)], m_send.at[k, s], m_recv.at[k, s], to)
                for k, (j, to) in enumerate(zip(froms, (right, left, across)))]

    def first_product(s, carry):
        slot = lax.rem(s, 2)
        x_copy(s + 1).start()

        @pl.when(s + 1 < nseq)
        def _():
            for c in a_copies(s + 1):
                c.start()

        @pl.when(s == nseq // 2)
        def _():
            pack_start(1)

        x_copy(s).wait()
        rms_rows(xbuf.at[slot], hbuf, gain, rows, 32)
        for c in a_copies(s):
            c.wait()
        mids[s, rank_rows(chip), :] = dot_nt(abuf[slot], hbuf[...]).astype(BF16)
        for c in mid_copies(s):
            c.start()
        return carry

    lax.fori_loop(0, nseq, first_product, 0)
    pack_start(2)
    for c in near[1:]:
        c.wait()
    for c in b_copies(0):
        c.start()
    for c in far:
        c.start()
    for c in mine:
        c.wait()

    half = rows // 2

    def out_right(s):
        return remote(attb.at[lax.rem(s, 2)], att.at[s, chip], r_send.at[lax.rem(s, 2)], rl_recv.at[s], right)

    def out_left(s):
        return remote(attb.at[lax.rem(s, 2)], att.at[s, chip], l_send.at[lax.rem(s, 2)], rr_recv.at[s], left)

    def out_own(s):
        return local(attb.at[lax.rem(s, 2)], att.at[s, chip], own_sem.at[lax.rem(s, 2)])

    def in_left(s):
        return remote(attb.at[0], att.at[s, before], r_send.at[0], rl_recv.at[s], right)

    def in_right(s):
        return remote(attb.at[0], att.at[s, after], l_send.at[0], rr_recv.at[s], left)

    def pass_right(s):
        part = att.at[s, before, pl.ds(0, half)]
        return remote(part, part, fr_send.at[s], fl_recv.at[s], right)

    def pass_left(s):
        part = att.at[s, after, pl.ds(half, half)]
        return remote(part, part, fl_send.at[s], fr_recv.at[s], left)

    def forward(s):
        in_left(s).wait_recv()
        pass_right(s).start()
        in_right(s).wait_recv()
        pass_left(s).start()

    def body(s, carry):
        g, slot = nseq + s, lax.rem(s, 2)

        @pl.when(s + 1 < nseq)
        def _():
            x_copy(g + 1).start()
            for c in b_copies(s + 1):
                c.start()

        x_copy(g).wait()
        rms_rows(xbuf.at[lax.rem(g, 2)], hbuf, gain, rows, 32)
        for c in mid_copies(s, (before, after, opposite)):
            c.wait_recv()
        mid = dot(sel[...], mids[s]).T.astype(BF16)
        for c in b_copies(s):
            c.wait()
        for p in range(3):
            z = dot_nt(hbuf[...], wbuf[pl.ds(p * width, width), :])
            z = z + scale * dot(mid, bbuf[slot, p])
            qkv[:, pl.ds(p * width, width)] = z.astype(BF16)

        @pl.when((s >= 2) & (s - 2 < keep))
        def _():
            out_right(s - 2).wait_send()
            out_left(s - 2).wait_send()

        @pl.when(s >= 2)
        def _():
            out_own(s - 2).wait()

        attend(qkv, attb.at[slot], width, group, dim, rows // 2)
        out_own(s).start()

        @pl.when(s < keep)
        def _():
            out_right(s).start()
            out_left(s).start()

        for k in range(len(packs)):
            @pl.when(s == k)
            def _(k=k):
                pack_pass(k)

        @pl.when((s >= lag) & (s - lag < keep))
        def _():
            forward(s - lag)

        return carry

    lax.fori_loop(0, nseq, body, 0)
    for k in range(len(packs)):
        pack_across(k)

    def tail(s, carry):
        forward(s)
        return carry

    lax.fori_loop(min(nseq - lag, keep), keep, tail, 0)
    for s in (nseq - 2, nseq - 1):
        if s < keep:
            out_right(s).wait_send()
            out_left(s).wait_send()
        out_own(s).wait()

    def finish(s, carry):
        pass_right(s).wait_send()
        pass_left(s).wait_send()
        got_a, got_b = att.at[s, opposite, pl.ds(0, half)], att.at[s, opposite, pl.ds(half, half)]
        remote(got_a, got_a, fr_send.at[s], fl_recv.at[s], right).wait_recv()
        remote(got_b, got_b, fl_send.at[s], fr_recv.at[s], left).wait_recv()
        return carry

    lax.fori_loop(0, keep, finish, 0)

    def finish_mids(s, carry):
        for c in mid_copies(s):
            c.wait_send()
        return carry

    lax.fori_loop(0, nseq, finish_mids, 0)
    for k in range(len(packs)):
        pack_end(k)
    for c in far:
        c.wait()


def call_a(n, keep, scale, group, dim, share, x, gain, wq, wk, wv, ar, bqkv, wide, agu, wo, wg, wu, wd, lml):
    nseq, rows, model = x.shape[0] // CORES, x.shape[1], x.shape[2]
    own = wq.shape[0]
    width = own * CORES
    rank3, arows = bqkv.shape[1], ar.shape[1]
    crows = CORES * arows
    hbm = pl.BlockSpec(memory_space=pl.ANY)
    vmem = pl.BlockSpec(memory_space=pltpu.VMEM)
    dma = pltpu.SemaphoreType.DMA
    lag = min(3, nseq)
    flops = 2 * nseq * rows * model * (3 * width + rank3)
    return pl.pallas_call(
        functools.partial(kernel_a, n, lag, keep, scale, group, dim, share),
        out_shape=[
            jax.ShapeDtypeStruct((nseq, n, rows, width), BF16),
            jax.ShapeDtypeStruct((nseq, *ar.shape[1:]), BF16),
            jax.ShapeDtypeStruct((nseq, *bqkv.shape[1:]), BF16),
            jax.ShapeDtypeStruct((n, CORES, *wide.shape), BF16),
            jax.ShapeDtypeStruct((n, CORES, *agu.shape), BF16),
            jax.ShapeDtypeStruct((n, CORES, *wo.shape), BF16),
            jax.ShapeDtypeStruct(wg.shape, BF16),
            jax.ShapeDtypeStruct(wu.shape, BF16),
            jax.ShapeDtypeStruct(wd.shape, BF16),
            jax.ShapeDtypeStruct((nseq, *lml.shape[1:]), BF16),
        ],
        in_specs=[hbm, vmem] + [hbm] * 12,
        out_specs=[hbm] * 10,
        scratch_shapes=[
            pltpu.VMEM((3 * width, model), BF16),
            pltpu.VMEM((2, rows, model), BF16),
            pltpu.VMEM((rows, model), BF16),
            pltpu.VMEM((2, crows, model), BF16),
            pltpu.VMEM((2, 3, rank3, width), BF16),
            pltpu.VMEM((rows, 3 * width), BF16),
            pltpu.VMEM((2, rows, width), BF16),
            pltpu.VMEM((nseq, n * crows, rows), BF16),
            pltpu.VMEM((rank3, n * crows), BF16),
            dma((3,)), dma((2,)), dma((2, 2)), dma((2, 3)), dma((2, 3)), dma((5,)), dma((5,)), dma((4,)), dma((4,)),
            dma((3, nseq)), dma((3, nseq)),
        ] + [dma((3,))] * 11 + [
            dma((2,)), dma((2,)), dma((2,)), dma((nseq,)), dma((nseq,)), dma((nseq,)), dma((nseq,)), dma((nseq,)), dma((nseq,)),
        ],
        compiler_params=pltpu.CompilerParams(collective_id=0, has_side_effects=True, vmem_limit_bytes=VMEM_LIMIT),
        cost_estimate=pl.CostEstimate(flops=flops, bytes_accessed=3 * x.size, transcendentals=nseq * rows * rows * width // dim),
        name="qkv_attention",
    )(x, gain, wq, wk, wv, ar, bqkv, wide, agu, wo, wg, wu, wd, lml)


def kernel_b(n, keep, scale, rank, share,
             x, gain, att, wo, wide, agu, wg, wg_o, wu, wu_o, wd, wd_o, lml, lml_o,
             y, att_t,
             wob, gub, wdb, attv, xb, hb, mb, zb, x1b, yb, in1l, in1r, in2l, in2r, aob, bob, agub, lgb, lub, adb, bdb, sel,
             wo_sem, gu_sem, wd_sem, att_sem, x_sem, lo_sem, lg_sem, bd_sem,
             s1r, s1l, s2r, s2l, ar, al, yown, fr, fl, r1l, r1r, r2l, r2r, gl, gr, hl, hr, dsend, drecv,
             t_rs, t_ls, t_rl, t_rr, t_frs, t_fls, t_fl, t_fr):
    core, chip, right, left, partner = ring(n)
    nseq, rows, model = att.shape[0], x.shape[1], x.shape[2]
    width = att.shape[3]
    ff = wg.shape[1]
    first = core * nseq
    ndev, piece_w = wide.shape[0], wide.shape[3]
    late = nseq - keep
    blk = rows // n
    half = blk // 2
    before, after, opposite = lax.rem(chip + n - 1, n), lax.rem(chip + 1, n), lax.rem(chip + 2, n)
    wo_t, gu_t, wd_t = wob.shape[2], gub.shape[3], wdb.shape[2]
    wo_n, gu_n, wd_n = model // wo_t, ff // gu_t, model // wd_t
    greet(right, left, partner)

    def wo_copy(k):
        at = pl.ds(pl.multiple_of(k * wo_t, wo_t), wo_t)
        return local(wo.at[:, at], wob.at[lax.rem(k, 2)], wo_sem.at[lax.rem(k, 2)])

    def gu_copies(k, own):
        at = pl.ds(pl.multiple_of(lax.rem(k, gu_n) * gu_t, gu_t), gu_t)
        slot = lax.rem(k, 2)
        pair = (wg, wu) if own else (wg_o, wu_o)
        return [local(w.at[:, at], gub.at[slot, j], gu_sem.at[slot, j]) for j, w in enumerate(pair)]

    def gu_start(k):
        @pl.when(k < gu_n)
        def _():
            for c in gu_copies(k, True):
                c.start()

        @pl.when(k >= gu_n)
        def _():
            for c in gu_copies(k, False):
                c.start()

    def wd_copies(k):
        at = pl.ds(pl.multiple_of(k * wd_t, wd_t), wd_t)
        slot = lax.rem(k, 2)
        return [local(w.at[:, at], wdb.at[slot, pl.ds(j * ff, ff)], wd_sem.at[slot, j]) for j, w in enumerate((wd, wd_o))]

    def att_copies(s):
        return [local(att.at[s, j], attv.at[:, pl.ds(j * width, width)], att_sem.at[j]) for j in range(n)]

    def att_start(s):
        @pl.when(s < keep)
        def _():
            start(att_copies(s))

        @pl.when(s >= keep)
        def _():
            k = jnp.maximum(s - keep, 0)
            late_in(k)
            for j, own in enumerate(att_copies(s)):
                @pl.when(chip == j)
                def _(own=own):
                    own.start()

                @pl.when(chip != j)
                def _(j=j):
                    local(att_t.at[k, j], attv.at[:, pl.ds(j * width, width)], att_sem.at[j]).start()

    def late_right(k):
        return remote(att.at[keep + k, chip], att_t.at[k, chip], t_rs.at[k], t_rl.at[k], right)

    def late_left(k):
        return remote(att.at[keep + k, chip], att_t.at[k, chip], t_ls.at[k], t_rr.at[k], left)

    def late_hops(k):
        a, b = att_t.at[k, before, pl.ds(0, rows // 2)], att_t.at[k, after, pl.ds(rows // 2, rows // 2)]
        return remote(a, a, t_frs.at[k], t_fl.at[k], right), remote(b, b, t_fls.at[k], t_fr.at[k], left)

    def late_pass(k):
        hop_r, hop_l = late_hops(k)
        remote(att.at[keep + k, chip], att_t.at[k, before], t_rs.at[k], t_rl.at[k], right).wait_recv()
        hop_r.start()
        remote(att.at[keep + k, chip], att_t.at[k, after], t_ls.at[k], t_rr.at[k], left).wait_recv()
        hop_l.start()

    def late_in(k):
        a, b = att_t.at[k, opposite, pl.ds(0, rows // 2)], att_t.at[k, opposite, pl.ds(rows // 2, rows // 2)]
        remote(a, a, t_frs.at[k], t_fl.at[k], right).wait_recv()
        remote(b, b, t_fls.at[k], t_fr.at[k], left).wait_recv()

    def x_copy(s):
        return local(x.at[first + s], xb, x_sem)

    def lora_o(s):
        slot, out = lax.rem(s, 2), []
        for d in range(ndev):
            cols = pl.ds(d * piece_w, piece_w)
            out.append(local(wide.at[d, first + s, pl.ds(0, rank)], aob.at[slot, :, cols], lo_sem.at[slot, 0, d]))
            out.append(local(wide.at[d, first + s, pl.ds(rank, rank)], bob.at[slot, :, cols], lo_sem.at[slot, 1, d]))
            out.append(local(agu.at[d, first + s], agub.at[slot, pl.ds(d * 2 * share, 2 * share)], lo_sem.at[slot, 2, d]))
        return out

    def lora_m(s):
        slot, out = lax.rem(s, 2), []
        for j, (src, k) in enumerate(((lml, first + s), (lml_o, s))):
            at = pl.ds(j * ff, ff)
            out.append(local(src.at[k, pl.ds(0, rank)], lgb.at[slot, pl.ds(0, rank), at], lg_sem.at[slot, 3 * j]))
            out.append(local(src.at[k, pl.ds(rank, rank)], lub.at[slot, pl.ds(rank, rank), at], lg_sem.at[slot, 3 * j + 1]))
            out.append(local(src.at[k, pl.ds(2 * rank, rank)], adb.at[slot, pl.ds(0, rank), at], lg_sem.at[slot, 3 * j + 2]))
        return out

    def start(copies):
        for c in copies:
            c.start()

    def wait(copies):
        for c in copies:
            c.wait()

    def rows_of(j, size=blk, shift=0):
        return pl.ds(pl.multiple_of(j * blk + shift, size), size)

    def rs1_right(s):
        return remote(zb.at[lax.rem(s, 3), rows_of(opposite, half)], in1l.at[lax.rem(s, 3)], s1r.at[s], r1l.at[s], right)

    def rs1_left(s):
        return remote(zb.at[lax.rem(s, 3), rows_of(opposite, half, half)], in1r.at[lax.rem(s, 3)], s1l.at[s], r1r.at[s], left)

    def rs2_right(s):
        return remote(zb.at[lax.rem(s, 3), rows_of(after)], in2l.at[lax.rem(s, 3)], s2r.at[s], r2l.at[s], right)

    def rs2_left(s):
        return remote(zb.at[lax.rem(s, 3), rows_of(before)], in2r.at[lax.rem(s, 3)], s2l.at[s], r2r.at[s], left)

    def ag1_right(s):
        return remote(yb.at[lax.rem(s, 2)], y.at[first + s, rows_of(chip)], ar.at[s], gl.at[s], right)

    def ag1_left(s):
        return remote(yb.at[lax.rem(s, 2)], y.at[first + s, rows_of(chip)], al.at[s], gr.at[s], left)

    def ag1_own(s):
        return local(yb.at[lax.rem(s, 2)], y.at[first + s, rows_of(chip)], yown.at[s])

    def ag2_right(s, block):
        part = y.at[first + s, rows_of(block, half)]
        return remote(part, part, fr.at[s], hl.at[s], right)

    def ag2_left(s, block):
        part = y.at[first + s, rows_of(block, half, half)]
        return remote(part, part, fl.at[s], hr.at[s], left)

    def across(s, k, block):
        part = y.at[first + s, rows_of(block)]
        return remote(yb.at[lax.rem(s, 2)] if k == 0 else part, part, dsend.at[k, s], drecv.at[k, s], partner)

    def across_in(s, k):
        there = y.at[(1 - core) * nseq + s, rows_of((chip, before, after, opposite)[k])]
        return remote(there, there, dsend.at[k, s], drecv.at[k, s], partner)

    def do_rs2(s):
        slot = lax.rem(s, 3)
        rs1_right(s).wait_recv()
        at = rows_of(after, half)
        zb[slot, at, :] = (zb[slot, at, :].astype(F32) + in1l[slot].astype(F32)).astype(BF16)
        rs2_right(s).start()
        rs1_left(s).wait_recv()
        at = rows_of(before, half, half)
        zb[slot, at, :] = (zb[slot, at, :].astype(F32) + in1r[slot].astype(F32)).astype(BF16)
        rs2_left(s).start()

    def do_rs3(s):
        slot, yslot = lax.rem(s, 3), lax.rem(s, 2)

        @pl.when(s >= 2)
        def _():
            ag1_right(s - 2).wait_send()
            ag1_left(s - 2).wait_send()
            ag1_own(s - 2).wait()
            across(s - 2, 0, chip).wait_send()

        rs2_right(s).wait_recv()
        rs2_left(s).wait_recv()
        mine = zb.at[slot, rows_of(chip)]
        tail = pl.ds(model, 128)
        mid = mine[:, tail].astype(F32) + in2l[slot, :, tail].astype(F32) + in2r[slot, :, tail].astype(F32)
        mid = mid.astype(BF16)[:, :rank]

        def piece(k, carry):
            at = pl.ds(pl.multiple_of(k * wo_t, wo_t), wo_t)
            z = mine[:, at].astype(F32) + in2l[slot, :, at].astype(F32) + in2r[slot, :, at].astype(F32)
            z = z + scale * dot(mid, bdb[s, :, at])
            yb[yslot, :, at] = (x1b[slot, :, at].astype(F32) + z).astype(BF16)
            return carry

        lax.fori_loop(0, wo_n, piece, 0)
        ag1_right(s).start()
        ag1_left(s).start()
        ag1_own(s).start()
        across(s, 0, chip).start()

    def do_ag2(s):
        remote(yb.at[0], y.at[first + s, rows_of(before)], ar.at[s], gl.at[s], right).wait_recv()
        ag2_right(s, before).start()
        across(s, 1, before).start()
        remote(yb.at[0], y.at[first + s, rows_of(after)], al.at[s], gr.at[s], left).wait_recv()
        ag2_left(s, after).start()
        across(s, 2, after).start()

    def do_across(s):
        ag2_right(s, opposite).wait_recv()
        ag2_left(s, opposite).wait_recv()
        across(s, 3, opposite).start()

    def when(cond, f, s):
        @pl.when(cond)
        def _():
            f(s)

    for k in range(late):
        late_right(k).start()
        late_left(k).start()
    bd_copies = [local(wide.at[d, pl.ds(first, nseq), pl.ds(2 * rank, rank)], bdb.at[:, :, pl.ds(d * piece_w, piece_w)],
                       bd_sem.at[d]) for d in range(ndev)]
    start(bd_copies)
    sel[...] = pick(sel.shape, share, rank, 2, 0)
    for k in range(2):
        wo_copy(k).start()
        start(gu_copies(k, True))
        start(wd_copies(k))
    start(att_copies(0))
    x_copy(0).start()
    start(lora_o(0))
    lgb[...] = jnp.zeros_like(lgb)
    lub[...] = jnp.zeros_like(lub)
    adb[...] = jnp.zeros_like(adb)
    start(lora_m(0))
    wait(bd_copies)

    def out_proj(s):
        slot = lax.rem(s, 2)
        wait(lora_o(s))
        wait(att_copies(s))
        x_copy(s).wait()
        mid = dot_nt(attv[...], aob[slot]).astype(BF16)

        def tile(k, carry):
            at = pl.ds(pl.multiple_of(k * wo_t, wo_t), wo_t)
            wo_copy(k).wait()
            z = dot(attv[...], wob[lax.rem(k, 2)]) + scale * dot(mid, bob[slot, :, at])
            xb[:, at] = (xb[:, at].astype(F32) + z).astype(BF16)

            @pl.when((k + 2 < wo_n) | (s + 1 < nseq))
            def _():
                wo_copy(lax.rem(k + 2, wo_n)).start()

            return carry

        lax.fori_loop(0, wo_n, tile, 0)
        rms_rows(xb, hb, gain, rows, 32)
        x1b[lax.rem(s, 3)] = xb[rows_of(chip), :]

        @pl.when(s + 1 < nseq)
        def _():
            att_start(s + 1)
            x_copy(s + 1).start()

    def gate_up(s):
        slot = lax.rem(s, 2)
        mid = dot_nt(hb[...], agub[slot]).astype(BF16)
        mid = dot(mid, sel[...]).astype(BF16)

        @pl.when(s + 1 < nseq)
        def _():
            start(lora_o(s + 1))

        wait(lora_m(s))

        def tile(k, carry):
            at = pl.ds(pl.multiple_of(k * gu_t, gu_t), gu_t)
            wait(gu_copies(k, True))
            g = dot(hb[...], gub[lax.rem(k, 2), 0]) + scale * dot(mid, lgb[slot, :, at])
            u = dot(hb[...], gub[lax.rem(k, 2), 1]) + scale * dot(mid, lub[slot, :, at])
            g = g.astype(BF16).astype(F32)
            u = u.astype(BF16).astype(F32)
            mb[:, at] = (jax.nn.silu(g) * u).astype(BF16)

            @pl.when((k + 2 < 2 * gu_n) | (s + 1 < nseq))
            def _():
                gu_start(lax.rem(k + 2, 2 * gu_n))

            return carry

        lax.fori_loop(0, 2 * gu_n, tile, 0)

        @pl.when(s + 1 < nseq)
        def _():
            start(lora_m(s + 1))

    def down(s):
        slot = lax.rem(s, 3)

        @pl.when(s >= 3)
        def _():
            rs1_right(s - 3).wait_send()
            rs1_left(s - 3).wait_send()
            rs2_right(s - 3).wait_send()
            rs2_left(s - 3).wait_send()

        zb[slot, :, pl.ds(model, 128)] = dot_nt(mb[...], adb[lax.rem(s, 2)]).astype(BF16)

        def tile(k, carry):
            at = pl.ds(pl.multiple_of(k * wd_t, wd_t), wd_t)
            wait(wd_copies(k))
            zb[slot, :, at] = dot(mb[...], wdb[lax.rem(k, 2)]).astype(BF16)

            @pl.when((k + 2 < wd_n) | (s + 1 < nseq))
            def _():
                start(wd_copies(lax.rem(k + 2, wd_n)))

            return carry

        lax.fori_loop(0, wd_n, tile, 0)
        rs1_right(s).start()
        rs1_left(s).start()

    def body(t, carry):
        when((t >= 4) & (t < nseq + 4), do_across, t - 4)
        when((t >= 3) & (t < nseq + 3), do_ag2, t - 3)
        when(t < nseq, out_proj, t)
        when((t >= 1) & (t < nseq + 1), do_rs2, t - 1)
        when(t < nseq, gate_up, t)
        if late > 0:
            when(t == 0, lambda _: late_pass(0), t)
        when((t >= 2) & (t < nseq + 2), do_rs3, t - 2)
        when(t < nseq, down, t)
        for k in range(1, late):
            when(t == k - 1, lambda _, k=k: late_pass(k), t)
        return carry

    lax.fori_loop(0, nseq + 4, body, 0)

    for s in range(max(nseq - 3, 0), nseq):
        rs1_right(s).wait_send()
        rs1_left(s).wait_send()
        rs2_right(s).wait_send()
        rs2_left(s).wait_send()
    for s in range(max(nseq - 2, 0), nseq):
        ag1_right(s).wait_send()
        ag1_left(s).wait_send()
        ag1_own(s).wait()
        across(s, 0, chip).wait_send()

    def finish(s, carry):
        ag2_right(s, before).wait_send()
        ag2_left(s, after).wait_send()
        for k, block in ((1, before), (2, after), (3, opposite)):
            across(s, k, block).wait_send()
        for k in range(4):
            across_in(s, k).wait_recv()
        return carry

    lax.fori_loop(0, nseq, finish, 0)
    for k in range(late):
        late_right(k).wait_send()
        late_left(k).wait_send()
        for hop in late_hops(k):
            hop.wait_send()


def call_b(n, keep, scale, rank, share, x, gain, att, wo, wide, agu, wg, wg_o, wu, wu_o, wd, wd_o, lml, lml_o):
    nseq, rows, model, ff = att.shape[0], x.shape[1], x.shape[2], wg.shape[1]
    hbm = pl.BlockSpec(memory_space=pl.ANY)
    vmem = pl.BlockSpec(memory_space=pltpu.VMEM)
    dma = pltpu.SemaphoreType.DMA
    blk = rows // n
    ndev = wide.shape[0]
    zwide = model + 128
    tile = 512
    flops = 2 * nseq * rows * (model * model + 3 * model * ff * CORES)
    return pl.pallas_call(
        functools.partial(kernel_b, n, keep, scale, rank, share),
        out_shape=[jax.ShapeDtypeStruct(x.shape, BF16), jax.ShapeDtypeStruct((nseq - keep, *att.shape[1:]), BF16)],
        in_specs=[hbm, vmem] + [hbm] * 12,
        out_specs=[hbm] * 2,
        scratch_shapes=[
            pltpu.VMEM((2, model, tile), BF16),
            pltpu.VMEM((2, 2, model, tile // 2), BF16),
            pltpu.VMEM((2, CORES * ff, tile), BF16),
            pltpu.VMEM((rows, model), BF16),
            pltpu.VMEM((rows, model), BF16),
            pltpu.VMEM((rows, model), BF16),
            pltpu.VMEM((rows, CORES * ff), BF16),
            pltpu.VMEM((3, rows, zwide), BF16),
            pltpu.VMEM((3, blk, model), BF16),
            pltpu.VMEM((2, blk, model), BF16),
            pltpu.VMEM((3, blk // 2, zwide), BF16),
            pltpu.VMEM((3, blk // 2, zwide), BF16),
            pltpu.VMEM((3, blk, zwide), BF16),
            pltpu.VMEM((3, blk, zwide), BF16),
            pltpu.VMEM((2, rank, model), BF16),
            pltpu.VMEM((2, rank, model), BF16),
            pltpu.VMEM((2, 2 * rank, model), BF16),
            pltpu.VMEM((2, 2 * rank, CORES * ff), BF16),
            pltpu.VMEM((2, 2 * rank, CORES * ff), BF16),
            pltpu.VMEM((2, 128, CORES * ff), BF16),
            pltpu.VMEM((nseq, rank, model), BF16),
            pltpu.VMEM((2 * rank, 2 * rank), BF16),
            dma((2,)), dma((2, 2)), dma((2, 2)), dma((n,)), dma, dma((2, 3, ndev)), dma((2, 6)), dma((ndev,)),
        ] + [dma((nseq,))] * 17 + [dma((4, nseq))] * 2 + [dma((nseq - keep,))] * 8,
        compiler_params=pltpu.CompilerParams(collective_id=1, has_side_effects=True, vmem_limit_bytes=VMEM_LIMIT),
        cost_estimate=pl.CostEstimate(flops=flops, bytes_accessed=4 * x.size, transcendentals=0),
        name="out_mlp",
    )(x, gain, att, wo, wide, agu, wg, wg_o, wu, wu_o, wd, wd_o, lml, lml_o)[0]


def solution(mesh):
    n = mesh.shape["tp"] // CORES
    act_spec = P("dp", None, None)
    w_head, w_out, w_col, w_row = P(None, "tp", None), P("tp", None, None), P(None, "tp"), P("tp", None)
    a_rank, b_head, b_col = P(None, None, "tp"), P(None, None, "tp", None), P(None, None, "tp")
    a_head, a_row = P(None, "tp", None, None), P(None, "tp", None)
    in_specs = (act_spec, P("dp"), P(None), P(None), w_head, w_head, w_head, w_out, w_col, w_col, w_row,
                a_rank, b_head, a_rank, b_head, a_rank, b_head, a_head, b_col, a_rank, b_col, a_rank, b_col, a_row, b_col)

    def local_layer(x_in, adapter_ids, gain_attn, gain_mlp, w_q, w_k, w_v, w_o, w_gate, w_up, w_down,
                    a_q, b_q, a_k, b_k, a_v, b_v, a_o, b_o, a_gate, b_gate, a_up, b_up, a_down, b_down):
        nseq, model = x_in.shape[0], x_in.shape[2]
        rank, dim = b_q.shape[1], w_q.shape[2]
        own = w_q.shape[1] * dim
        scale = LORA_ALPHA / rank
        share = a_q.shape[2]
        group = math.lcm(dim, 128) // dim
        keep = max(nseq // CORES - 2, 1)

        def take(*stacks):
            return jnp.take(jnp.concatenate(stacks, axis=1), adapter_ids, axis=0, mode="clip")

        def turn(stack):
            return jnp.swapaxes(stack, 1, 2)

        ar = take(turn(a_q), turn(a_k), turn(a_v), jnp.zeros((a_q.shape[0], share, model), BF16))
        bqkv = take(*[b.reshape(-1, rank, own) for b in (b_q, b_k, b_v)])
        wide = take(turn(a_o.reshape(-1, own, rank)), b_o, b_down)
        agu = take(turn(a_gate), turn(a_up))
        lml = take(b_gate, b_up, turn(a_down))
        flat = [jnp.transpose(w, (1, 2, 0)).reshape(own, model) for w in (w_q, w_k, w_v)]
        att, _, _, wide_f, agu_f, wo_f, wg_o, wu_o, wd_o, lml_o = call_a(
            n, keep, scale, group, dim, share, x_in, gain_attn.reshape(1, model), *flat, ar, bqkv, wide, agu,
            w_o.reshape(own, model), w_gate, w_up, w_down, lml)
        return call_b(n, keep, scale, rank, share, x_in, gain_mlp.reshape(1, model), att, wo_f.reshape(-1, model),
                      wide_f.reshape(-1, *wide.shape), agu_f.reshape(-1, *agu.shape), w_gate, wg_o, w_up, wu_o, w_down, wd_o,
                      lml, lml_o)

    return jax.shard_map(local_layer, mesh=mesh, in_specs=in_specs, out_specs=act_spec, check_vma=False)
```

time: 1830 us -> 858 us (0.47)
  waiting for transfers between devices: 944 us -> 0 us
  Pallas kernels: 0 us -> 806 us
  matrix products: 555 us -> 0 us
  blocking collectives: 104 us -> 0 us
  other arithmetic: 94.1 us -> 4.09 us
  local copies, waits for them, and re-layouts: 111 us -> 47.6 us
    pallas_call x0 -> x2, Pallas kernels: none -> 806 us  [the longest x1 496 us: call_b(): pl.pallas_call(functools.partial(kernel_b, n, keep, scale, rank, share),...]
    dot_general x23 -> x0, matrix products: 555 us -> none  [the longest x5 222 us: column_proj(): jnp.einsum('bsd,de->bse', h_in, w_loc, preferred_element_type=jnp.float32)]
    reduce_scatter x2 -> x0, waiting for transfers between devices: 498 us -> none  [row_proj(): lax.psum_scatter(base_part, 'tp', scatter_dimension=2, tiled=True)]
    all_gather x2 -> x0, waiting for transfers between devices: 440 us -> none  [row_proj(): lax.all_gather(out_loc.astype(jnp.bfloat16), 'tp', axis=2, tiled=True)]
    all_gather x5 -> x0, blocking collectives: 104 us -> none  [column_proj(): value_a8 = lax.all_gather(value_a9, 'tp', axis=2, tiled=True)]
    all_gather x1 -> x0, local copies, waits for them, and re-layouts: 64.5 us -> none  [row_proj(): lax.all_gather(out_loc.astype(jnp.bfloat16), 'tp', axis=2, tiled=True)]
    reduce_sum x3 -> x0, other arithmetic: 55 us -> none  [the longest x2 32.6 us: rms_scale(): jnp.mean(x_f32 * x_f32, axis=-1, keepdims=True) + RMS_EPS]
    convert_element_type x1 -> x0, other arithmetic: 33.9 us -> none  [rms_scale(): return (x_f32 * inv_rms * gain_vec).astype(jnp.bfloat16)]
  transfers between devices with their start and end apart: 6 -> 0, of which waited for: 5 -> 0; matrix products, arithmetic and copies ran while one was open for 7% -> 0% of each run, Pallas kernels for 0% -> 0%
where the time goes in v1:
time: 858 us; the launch traced here: 857 us
  Pallas kernels  806 us (94%)
  local copies, waits for them, and re-layouts  47.6 us (6%)
    pallas_call x1, Pallas kernels, call_b(): pl.pallas_call(functools.partial(kernel_b, n, keep, scale, rank, share),...  496 us
    pallas_call x1, Pallas kernels, call_a(): pl.pallas_call(functools.partial(kernel_a, n, lag, keep, scale, group, di...  309 us
    unnamed x18, local copies, waits for them, and re-layouts  33.6 us

profile of v1, /device:TPU:113, one launch (start us, length us, event | category | flops | bytes accessed | tf_op | source)
XLA Modules:
  0.0 857.4 jit_solution(10124258019328301856)
XLA Ops:
  0.0 0.1 pad.14.clone
  0.1 0.7 pad_clamp_fusion
  0.7 1.4 reshape.44
  2.2 1.4 reshape.45
  3.7 1.4 reshape.46
  5.1 0.0 copy-start
  5.1 0.1 pad_maximum_fusion.1
  5.2 0.0 copy-start.1
  5.3 1.7 gather_fusion.1
  7.0 0.3 copy.26
  7.3 0.4 reshape.47
  7.7 0.0 copy-start.4
  7.7 0.1 pad_maximum_fusion.2
  7.8 0.0 copy-start.5
  7.9 1.7 gather_fusion.2
  9.6 0.4 pad_maximum_fusion.3
  10.0 1.5 gather_fusion.3
  11.5 0.8 maximum_maximum_fusion
  12.2 1.8 gather_fusion
  14.1 2.0 pad_maximum_fusion
  16.1 2.4 gather_fusion.4
  18.5 309.2 %qkv_attention.1 = (bf16[8,4,512,768]{3,2,1,0:T(8,128)(2,1)}, bf16[8,16,3072]{2,1,0:T(8,128)(2,1)}, bf16[8,96,384]{2,1,0:T(8,128)(2,1)}, bf16[4,2,16,96,384]{4,3...) custom-call(bf16[16,512,3072]{2,1,0:T(8,128)(2,1)} %x.3, ...), custom_call_target="tpu_custom_call" | custom-call | flops 60397977600 | bytes 75497472 | tf_op jit(solution)/shard_map/qkv_attention/pallas_call | solution.py:388
  327.7 496.4 %out_mlp.1 = (bf16[16,512,3072]{2,1,0:T(8,128)(2,1)}, bf16[2,4,512,768]{3,2,1,0:T(8,128)(2,1)}) custom-call(bf16[16,512,3072]{2,1,0:T(8,128)(2,1)} %x.3, f32[1,3072]{1,0:T(1,128)} %bitcast.36, bf16[8,4,512,768]{3,2,1,0:T(8,128)(2,1)} %get-tuple-element.14.att, bf16[3072,3072]{1,0:T(8,128)(2,1)} %bitcast.37, bf16[8,16,96,384]{3,2,1,0:T(8,128)(2,1)} %bitcast.38, ...), custom_call_target="tpu_custom_call" | custom-call | flops 231928233984 | bytes 100663296 | tf_op jit(solution)/shard_map/out_mlp/pallas_call | solution.py:804
  824.1 33.3 %copy.28 = bf16[16,512,3072]{2,1,0:T(8,128)(2,1)} copy(bf16[16,512,3072]{2,1,0:T(8,128)(2,1)} %get-tuple-element.22) | data formatting | bytes 100663296
  (13 shorter events, 0.0 us)
Async XLA Ops:
  5.1 1.9 copy-start
  5.2 2.4 copy-start.1
  5.3 2.4 copy-start.2
  7.7 1.9 copy-start.3
  7.7 1.9 copy-start.4
  7.8 3.6 copy-start.5
  7.8 3.6 copy-start.6
  7.9 3.6 copy-start.7

commit v2 on v1

v2 whole, which is shorter than its diff:
```python
import functools
import math

import jax
import jax.numpy as jnp
from jax import lax
from jax.experimental import pallas as pl
from jax.experimental.pallas import tpu as pltpu
from jax.sharding import PartitionSpec as P

LORA_ALPHA = 16
RMS_EPS = 1e-5
CORES = 2
MESH = pl.DeviceIdType.MESH
F32, BF16 = jnp.float32, jnp.bfloat16
NT = (((1,), (1,)), ((), ()))
VMEM_LIMIT = 67_000_000
PAIR, TRIPLE, QUAD = 2, 3, 4
LANES = 128
N = None


def even(k):
    return lax.rem(k, PAIR)


def third(k):
    return lax.rem(k, TRIPLE)


def head(size):
    return pl.ds(0, size)


def loop(count, body, start):
    return lax.fori_loop(0, count, body, start)


def dot(a, b):
    return jnp.dot(a, b, preferred_element_type=F32)


def dot_nt(a, b):
    return lax.dot_general(a, b, NT, preferred_element_type=F32)


def ring(n):
    me = lax.axis_index("tp")
    core, chip = lax.rem(me, CORES), lax.div(me, CORES)
    right = lax.rem(chip + 1, n) * CORES + core
    left = lax.rem(chip + n - 1, n) * CORES + core
    return core, chip, right, left, chip * CORES + 1 - core


def greet(*others):
    barrier = pltpu.get_barrier_semaphore()
    for other in others:
        pl.semaphore_signal(barrier, inc=1, device_id={"tp": other}, device_id_type=MESH)
    pl.semaphore_wait(barrier, len(others))


def remote(src, dst, send, recv, to):
    return pltpu.make_async_remote_copy(src_ref=src, dst_ref=dst, send_sem=send, recv_sem=recv, device_id={"tp": to},
                                        device_id_type=MESH)


def local(src, dst, sem):
    return pltpu.make_async_copy(src, dst, sem)


def rms_rows(src, dst, gain, rows, step):
    def chunk(k, carry):
        at = pl.ds(pl.multiple_of(k * step, step), step)
        v = src[at, :].astype(F32)
        inv = lax.rsqrt(jnp.mean(v * v, axis=-1, keepdims=True) + RMS_EPS)
        dst[at, :] = (v * inv * gain[...]).astype(BF16)
        return carry

    loop(rows // step, chunk, 0)


def head_windows(group, dim):
    out = []
    for h in range(group):
        lo, hi = h * dim, (h + 1) * dim
        start, stop = lo // 128 * 128, -(-hi // 128) * 128
        out.append((start, stop, lo - start, hi - start))
    return out


def attend(qkv, out, width, group, dim, qblock):
    seq = qkv.shape[0]
    lanes = group * dim

    def one_group(g, carry):
        base = pl.multiple_of(g * lanes, 128)
        for qb in range(seq // qblock):
            rows, keys = pl.ds(qb * qblock, qblock), (qb + 1) * qblock
            acc = [None] * (lanes // 128)
            mask = (lax.broadcasted_iota(jnp.int32, (qblock, keys), 0) + qb * qblock
                    >= lax.broadcasted_iota(jnp.int32, (qblock, keys), 1))
            for start, stop, lo, hi in head_windows(group, dim):
                size = stop - start
                lane_q = lax.broadcasted_iota(jnp.int32, (qblock, size), 1)
                lane_k = lax.broadcasted_iota(jnp.int32, (keys, size), 1)
                q = qkv[rows, pl.ds(base + start, size)]
                k = qkv[head(keys), pl.ds(width + base + start, size)]
                v = qkv[head(keys), pl.ds(2 * width + base + start, size)]
                q = jnp.where((lane_q >= lo) & (lane_q < hi), q, jnp.zeros_like(q))
                v = jnp.where((lane_k >= lo) & (lane_k < hi), v, jnp.zeros_like(v))
                scores = jnp.where(mask, dot_nt(q, k) * dim ** -0.5, -jnp.inf)
                top = jnp.max(scores, axis=-1, keepdims=True)
                e = jnp.exp(scores - top)
                prob = (e / jnp.sum(e, axis=-1, keepdims=True)).astype(BF16)
                o = dot(prob, v)
                for t in range(size // 128):
                    piece = o[:, t * 128:(t + 1) * 128]
                    j = start // 128 + t
                    acc[j] = piece if acc[j] is None else acc[j] + piece
            for j, piece in enumerate(acc):
                out[rows, pl.ds(base + j * 128, 128)] = piece.astype(BF16)
        return carry

    loop(width // lanes, one_group, 0)


def pick(shape, share, ranks, slots, axis):
    i = lax.broadcasted_iota(jnp.int32, shape, axis)
    t = lax.broadcasted_iota(jnp.int32, shape, 1 - axis)
    dev, slot, r = i // (slots * share), (i // share) % slots, i % share
    return jnp.where(t == slot * ranks + dev * share + r, 1.0, 0.0).astype(BF16)


class OutStage:
    def __init__(self, n, scale, rank, share, x, gain, wo_refs, wide_refs, agu_refs, bufs, wo_sem, lo_sem):
        self.core, self.chip, *_ = ring(n)
        self.before, self.after = lax.rem(self.chip + n - 1, n), lax.rem(self.chip + 1, n)
        self.opposite = lax.rem(self.chip + 2, n)
        self.scale, self.rank, self.share, self.x, self.gain = scale, rank, share, x, gain
        self.wide_refs, self.agu_refs, self.bufs = wide_refs, agu_refs, bufs
        self.wo_sem, self.lo_sem = wo_sem, lo_sem
        self.rows, self.first = x.shape[1], self.core * (x.shape[0] // CORES)
        wo, wo_l, wo_r, wo_f, wo_x = wo_refs
        hi, deep = wo_l.shape[0], wo.shape[0]
        self.width = wide_refs[0].shape[2]
        self.tile_w = bufs[0].shape[2]
        self.tiles_n = x.shape[2] // self.tile_w
        chips = (self.chip, self.before, self.after, self.opposite)
        self.shares = [(CORES * c + self.core, 0, j) for j, c in enumerate(chips)]
        self.shares += [(CORES * c + 1 - self.core, 1, j) for j, c in enumerate(chips)]
        self.wo_shares = []
        for d, cross, j in self.shares:
            base = pl.multiple_of(d * deep, deep)
            if cross or j in (0, 3):
                self.wo_shares.append((self.share_of((wo, wo_f, wo_x), cross, j), pl.ds(base, deep)))
            else:
                self.wo_shares.append(((wo_l, wo_r)[j - 1], pl.ds(base, hi)))
                self.wo_shares.append((wo_f.at[j - 1, pl.ds(hi, deep - hi)], pl.ds(base + hi, deep - hi)))

    @staticmethod
    def share_of(refs, cross, j):
        return refs[2].at[j] if cross else refs[0] if j == 0 else refs[1].at[j - 1]

    def cols(self, d):
        return pl.ds(pl.multiple_of(d * self.width, self.width), self.width)

    def wo_copies(self, k):
        wob = self.bufs[0]
        at, slot = pl.ds(pl.multiple_of(k * self.tile_w, self.tile_w), self.tile_w), even(k)
        return [local(src.at[:, at], wob.at[slot, rows_at], self.wo_sem.at[slot, j])
                for j, (src, rows_at) in enumerate(self.wo_shares)]

    def lora(self, s, slot):
        _, _, _, _, aob, bob, agub = self.bufs
        rank, out = self.rank, []
        for d, cross, j in self.shares:
            src = self.share_of(self.wide_refs, cross, j).at[s if cross else self.first + s]
            out.append(local(src.at[head(rank)], aob.at[slot, :, self.cols(d)], self.lo_sem.at[slot, 0, 4 * cross + j]))
            out.append(local(src.at[pl.ds(rank, rank)], bob.at[slot, :, self.cols(d)], self.lo_sem.at[slot, 1, 4 * cross + j]))
        for i, (j, src, k) in enumerate(((self.core, self.agu_refs[0], self.first + s), (1 - self.core, self.agu_refs[1], s))):
            rows_at = pl.ds(pl.multiple_of(j * 2 * self.share, 2 * self.share), 2 * self.share)
            out.append(local(src.at[k], agub.at[slot, rows_at], self.lo_sem.at[slot, 2, i]))
        return out

    def first_product(self, slot):
        _, attv, _, mido, aob, _, _ = self.bufs
        mido[...] = dot_nt(attv[...], aob[slot]).astype(BF16)

    def tiles(self, slot, lo, hi, more):
        wob, attv, xb, mido, _, bob, _ = self.bufs
        mid = mido[...]

        def tile(k, carry):
            at = pl.ds(pl.multiple_of(k * self.tile_w, self.tile_w), self.tile_w)
            for c in self.wo_copies(k):
                c.wait()
            z = dot(attv[...], wob[even(k)]) + self.scale * dot(mid, bob[slot, :, at])
            xb[:, at] = (xb[:, at].astype(F32) + z).astype(BF16)

            @pl.when((k + 2 < self.tiles_n) | more)
            def _():
                for c in self.wo_copies(lax.rem(k + 2, self.tiles_n)):
                    c.start()

            return carry

        lax.fori_loop(lo, hi, tile, 0)

    def norm(self, slot, h, mid_rows):
        _, _, xb, _, _, _, agub = self.bufs
        rms_rows(xb, h, self.gain, self.rows, 64)
        mid_rows[...] = dot_nt(agub[slot], h[...]).astype(BF16)


def kernel_a(n, lag, keep, scale, group, dim, share,
             x, gain, gain_mlp, wq, wk, wv, ar, agu, bqkv, wide, wo, wo_l, wo_r, wg, wu, wd, lml,
             att, ar_oth, agu_oth, b_oth, wide_f, wide_x, wo_f, wo_x, wg_o, wu_o, wd_o, lml_o, h_out, x1_out, mg_out,
             wbuf, xbuf, hbuf, abuf, bbuf, qkv, attb, mids, sel, wob, attv, xb, hb, mido, aob, bob, agub, mgu,
             w_sem, x_sem, a_sem, bo_sem, bp_sem, d_send, d_recv, o_send, o_recv, m_send, m_recv,
             pr_send, pl_send, prl_recv, prr_recv, pfr_send, pfl_send, pfl_recv, pfr_recv, pp_send, pp_recv,
             r_send, l_send, own_sem, rl_recv, rr_recv, fr_send, fl_send, fl_recv, fr_recv,
             wo_sem, lo_sem, att_sem, xo_sem, g_send, g_recv, e_sem):
    core, chip, right, left, partner = ring(n)
    before, after, opposite = lax.rem(chip + n - 1, n), lax.rem(chip + 1, n), lax.rem(chip + 2, n)
    across = opposite * CORES + core
    nseq, rows, own = x.shape[0] // CORES, x.shape[1], wq.shape[0]
    width = own * CORES
    first = core * nseq
    rank = bqkv.shape[1] // 3
    arows = ar.shape[1]
    crows = CORES * arows
    greet(right, left, partner, across)

    theirs, mine_at = pl.ds((1 - core) * nseq, nseq), pl.ds(first, nseq)
    near = [remote(ar.at[theirs], ar_oth, d_send.at[4], d_recv.at[4], partner)]
    near += [remote(w, wbuf.at[pl.ds(p * width + core * own, own)], d_send.at[p], d_recv.at[p], partner)
             for p, w in enumerate((wq, wk, wv))]
    near.append(remote(bqkv.at[theirs], b_oth, d_send.at[3], d_recv.at[3], partner))
    far = [remote(src, dst, o_send.at[k], o_recv.at[k], partner)
           for k, (src, dst) in enumerate(((lml.at[theirs], lml_o), (wg, wg_o), (wu, wu_o), (wd, wd_o),
                                     (agu.at[theirs], agu_oth)))]
    mine = [local(w, wbuf.at[pl.ds(p * width + core * own, own)], w_sem.at[p]) for p, w in enumerate((wq, wk, wv))]

    hi = wo_l.shape[0]
    whole, top, low = head(wo.shape[0]), head(hi), pl.ds(hi, wo.shape[0] - hi)
    wide_half = wide.shape[0] // 2
    to_right, to_left = (right, pr_send, prl_recv, pfr_send, pfl_recv), (left, pl_send, prr_recv, pfl_send, pfr_recv)

    def pack_first(k, way):
        to, send, recv, _, _ = (to_right, to_left)[way]
        if k == 0:
            return remote(wide, wide_f.at[way], send.at[k], recv.at[k], to)
        return remote(wo.at[low], wo_f.at[way, low], send.at[k], recv.at[k], to)

    def pack_second(k, way):
        to, _, _, send, recv = (to_right, to_left)[way]
        if k == 0:
            part = pl.ds(way * wide_half, wide_half)
            return remote(wide_f.at[way, part], wide_f.at[2, part], send.at[k], recv.at[k], to)
        part = (top, low)[way]
        return remote(wo_l if way == 0 else wo_f.at[1, low], wo_f.at[2, part], send.at[k], recv.at[k], to)

    def wide_push(j):
        src = wide if j == 0 else wide_f.at[j - 1]
        return remote(src.at[theirs], wide_x.at[j], pp_send.at[j], pp_recv.at[j], partner)

    def wo_push(j):
        src, dst = ((wo, wo_x.at[0]), (wo_l, wo_x.at[1, top]), (wo_r, wo_x.at[2, top]), (wo_f.at[0, low], wo_x.at[1, low]),
                    (wo_f.at[1, low], wo_x.at[2, low]), (wo_f.at[2], wo_x.at[3]))[j]
        return remote(src, dst, pp_send.at[4 + j], pp_recv.at[4 + j], partner)

    def pack_start(k):
        for way in range(2):
            pack_first(k, way).start()
        if k == 0:
            wide_push(0).start()
        else:
            for j in range(3):
                wo_push(j).start()

    def pack_pass(k):
        for way in range(2):
            pack_first(k, way).wait_recv()
            if k == 0 or way == 1:
                pack_second(k, way).start()
            (wide_push(way + 1) if k == 0 else wo_push(way + 3)).start()

    def pack_across(k):
        for way in range(2):
            pack_second(k, way).wait_recv()
        (wide_push(3) if k == 0 else wo_push(5)).start()

    def wo_ready():
        for j in range(4):
            wide_push(j).wait_recv()
        for j in range(6):
            wo_push(j).wait_recv()
        far[4].wait_recv()

    def pack_end():
        for k in range(2):
            for way in range(2):
                pack_first(k, way).wait_send()
                pack_second(k, way).wait_send()
        for j in range(4):
            wide_push(j).wait_send()
        for j in range(6):
            wo_push(j).wait_send()

    def x_copy(g):
        return local(x.at[first + lax.rem(g, nseq)], xbuf.at[even(g)], x_sem.at[even(g)])

    def a_copies(s):
        slot = even(s)
        own_at = pl.ds(pl.multiple_of(core * arows, arows), arows)
        oth_at = pl.ds(pl.multiple_of((1 - core) * arows, arows), arows)
        return [local(ar.at[first + s], abuf.at[slot, own_at], a_sem.at[slot, 0]),
                local(ar_oth.at[s], abuf.at[slot, oth_at], a_sem.at[slot, 1])]

    def b_copies(s):
        slot, out = even(s), []
        for p in range(3):
            part = pl.ds(p * rank, rank)
            own_at = pl.ds(pl.multiple_of(core * own, 128), own)
            oth_at = pl.ds(pl.multiple_of((1 - core) * own, 128), own)
            out.append(local(bqkv.at[first + s, part], bbuf.at[slot, p, part, own_at], bo_sem.at[slot, p]))
            out.append(local(b_oth.at[s, part], bbuf.at[slot, p, part, oth_at], bp_sem.at[slot, p]))
        return out

    near[0].start()
    pack_start(0)
    for c in near[1:] + mine:
        c.start()
    x_copy(0).start()
    bbuf[...] = jnp.zeros_like(bbuf)
    sel[...] = pick(sel.shape, share, rank, arows // share, 1)
    near[0].wait()
    for c in a_copies(0):
        c.start()

    def rank_rows(j):
        return pl.ds(pl.multiple_of(j * crows, crows), crows)

    def mid_copies(s, source=None):
        froms = (chip, chip, chip) if source is None else source
        return [remote(mids.at[s, rank_rows(j)], mids.at[s, rank_rows(j)], m_send.at[k, s], m_recv.at[k, s], to)
                for k, (j, to) in enumerate(zip(froms, (right, left, across)))]

    def first_product(s, carry):
        slot = even(s)
        x_copy(s + 1).start()

        @pl.when(s + 1 < nseq)
        def _():
            for c in a_copies(s + 1):
                c.start()

        @pl.when(s == nseq // 2)
        def _():
            pack_start(1)

        x_copy(s).wait()
        rms_rows(xbuf.at[slot], hbuf, gain, rows, 32)
        for c in a_copies(s):
            c.wait()
        mids[s, rank_rows(chip), :] = dot_nt(abuf[slot], hbuf[...]).astype(BF16)
        for c in mid_copies(s):
            c.start()
        return carry

    loop(nseq, first_product, 0)
    pack_second(1, 0).start()
    for c in near[1:]:
        c.wait()
    for c in b_copies(0):
        c.start()
    for c in far:
        c.start()
    for c in mine:
        c.wait()

    half = rows // 2

    def out_right(s):
        return remote(attb.at[even(s)], att.at[s, chip], r_send.at[even(s)], rl_recv.at[s], right)

    def out_left(s):
        return remote(attb.at[even(s)], att.at[s, chip], l_send.at[even(s)], rr_recv.at[s], left)

    def out_own(s):
        return local(attb.at[even(s)], att.at[s, chip], own_sem.at[even(s)])

    def in_left(s):
        return remote(attb.at[0], att.at[s, before], r_send.at[0], rl_recv.at[s], right)

    def in_right(s):
        return remote(attb.at[0], att.at[s, after], l_send.at[0], rr_recv.at[s], left)

    def pass_right(s):
        part = att.at[s, before, head(half)]
        return remote(part, part, fr_send.at[s], fl_recv.at[s], right)

    def pass_left(s):
        part = att.at[s, after, pl.ds(half, half)]
        return remote(part, part, fl_send.at[s], fr_recv.at[s], left)

    def forward(s):
        in_left(s).wait_recv()
        pass_right(s).start()
        in_right(s).wait_recv()
        pass_left(s).start()

    def gathered(s):
        got_a, got_b = att.at[s, opposite, head(half)], att.at[s, opposite, pl.ds(half, half)]
        remote(got_a, got_a, fr_send.at[s], fl_recv.at[s], right).wait_recv()
        remote(got_b, got_b, fl_send.at[s], fr_recv.at[s], left).wait_recv()

    grows = CORES * 2 * share
    blk = rows // n

    def group_rows(j):
        return pl.ds(pl.multiple_of(j * grows, grows), grows)

    def gate_mids(froms):
        return [remote(mgu.at[group_rows(j)], mgu.at[group_rows(j)], g_send.at[k], g_recv.at[k], to)
                for k, (j, to) in enumerate(zip(froms, (right, left, across)))]

    def exports():
        return [local(hb, h_out, e_sem.at[0]),
                local(xb.at[pl.ds(pl.multiple_of(chip * blk, blk), blk)], x1_out, e_sem.at[1])]

    def first_out():
        stage = OutStage(n, scale, rank, share, x, gain_mlp, (wo, wo_l, wo_r, wo_f, wo_x), (wide, wide_f, wide_x),
                         (agu, agu_oth), (wob, attv, xb, mido, aob, bob, agub), wo_sem, lo_sem)
        wo_ready()
        gathered(0)
        loads = [local(att.at[0, j], attv.at[:, pl.ds(j * width, width)], att_sem.at[j]) for j in range(n)]
        loads += [local(x.at[first], xb, xo_sem)] + stage.lora(0, 0)
        for c in loads + stage.wo_copies(0) + stage.wo_copies(1):
            c.start()
        for c in loads:
            c.wait()
        stage.first_product(0)
        stage.tiles(0, 0, stage.tiles_n, False)
        stage.norm(0, hb, mgu.at[group_rows(chip)])
        for c in gate_mids((chip, chip, chip)) + exports():
            c.start()

    def body(s, carry):
        g, slot = nseq + s, even(s)

        @pl.when(s + 1 < nseq)
        def _():
            x_copy(g + 1).start()
            for c in b_copies(s + 1):
                c.start()

        x_copy(g).wait()
        rms_rows(xbuf.at[even(g)], hbuf, gain, rows, 32)
        for c in mid_copies(s, (before, after, opposite)):
            c.wait_recv()
        mid = dot(sel[...], mids[s]).T.astype(BF16)
        for c in b_copies(s):
            c.wait()
        for p in range(3):
            z = dot_nt(hbuf[...], wbuf[pl.ds(p * width, width), :])
            z = z + scale * dot(mid, bbuf[slot, p])
            qkv[:, pl.ds(p * width, width)] = z.astype(BF16)

        @pl.when((s >= 2) & (s - 2 < keep))
        def _():
            out_right(s - 2).wait_send()
            out_left(s - 2).wait_send()

        @pl.when(s >= 2)
        def _():
            out_own(s - 2).wait()

        attend(qkv, attb.at[slot], width, group, dim, rows // 2)
        out_own(s).start()

        @pl.when(s < keep)
        def _():
            out_right(s).start()
            out_left(s).start()

        @pl.when(s == 0)
        def _():
            for k in range(2):
                pack_pass(k)


        @pl.when((s >= lag) & (s - lag < keep))
        def _():
            forward(s - lag)

        @pl.when(s == nseq - 2)
        def _():
            for k in range(2):
                pack_across(k)

        return carry

    loop(nseq, body, 0)

    def tail(s, carry):
        forward(s)
        return carry

    lax.fori_loop(max(min(nseq - lag, keep), 0), keep, tail, 0)
    first_out()
    for s in (nseq - 2, nseq - 1):
        if s < keep:
            out_right(s).wait_send()
            out_left(s).wait_send()
        out_own(s).wait()

    def finish(s, carry):
        pass_right(s).wait_send()
        pass_left(s).wait_send()

        @pl.when(s >= 1)
        def _():
            gathered(s)

        return carry

    loop(keep, finish, 0)

    def finish_mids(s, carry):
        for c in mid_copies(s):
            c.wait_send()
        return carry

    loop(nseq, finish_mids, 0)
    pack_end()
    for c in far[:4]:
        c.wait()
    far[4].wait_send()
    for c in gate_mids((before, after, opposite)):
        c.wait_recv()
    last = local(mgu, mg_out, e_sem.at[2])
    last.start()
    for c in gate_mids((chip, chip, chip)):
        c.wait_send()
    for c in exports() + [last]:
        c.wait()


def call_a(n, keep, scale, group, dim, share, x, gain, gain_mlp, wq, wk, wv, ar, agu, bqkv, wide, wo, wo_l, wo_r, wg, wu, wd, lml):
    nseq, rows, model = x.shape[0] // CORES, x.shape[1], x.shape[2]
    own = wq.shape[0]
    width = own * CORES
    rank3 = bqkv.shape[1]
    crows = CORES * ar.shape[1]
    hbm = pl.BlockSpec(memory_space=pl.ANY)
    vmem = pl.BlockSpec(memory_space=pltpu.VMEM)
    dma = pltpu.SemaphoreType.DMA
    lag = min(5, nseq)
    flops = 2 * nseq * rows * model * (3 * width + rank3)
    return pl.pallas_call(
        functools.partial(kernel_a, n, lag, keep, scale, group, dim, share),
        out_shape=[
            jax.ShapeDtypeStruct((nseq, n, rows, width), BF16),
            jax.ShapeDtypeStruct((nseq, *ar.shape[1:]), BF16),
            jax.ShapeDtypeStruct((nseq, *agu.shape[1:]), BF16),
            jax.ShapeDtypeStruct((nseq, *bqkv.shape[1:]), BF16),
            jax.ShapeDtypeStruct((n - 1, *wide.shape), BF16),
            jax.ShapeDtypeStruct((n, nseq, *wide.shape[1:]), BF16),
            jax.ShapeDtypeStruct((n - 1, *wo.shape), BF16),
            jax.ShapeDtypeStruct((n, *wo.shape), BF16),
            jax.ShapeDtypeStruct(wg.shape, BF16),
            jax.ShapeDtypeStruct(wu.shape, BF16),
            jax.ShapeDtypeStruct(wd.shape, BF16),
            jax.ShapeDtypeStruct((nseq, *lml.shape[1:]), BF16),
            jax.ShapeDtypeStruct((rows, model), BF16),
            jax.ShapeDtypeStruct((rows // n, model), BF16),
            jax.ShapeDtypeStruct((n * CORES * 2 * share, rows), BF16),
        ],
        in_specs=[hbm, vmem, vmem] + [hbm] * 14,
        out_specs=[hbm] * 15,
        scratch_shapes=[
            pltpu.VMEM((3 * width, model), BF16),
            pltpu.VMEM((PAIR, rows, model), BF16),
            pltpu.VMEM((rows, model), BF16),
            pltpu.VMEM((PAIR, crows, model), BF16),
            pltpu.VMEM((PAIR, 3, rank3, width), BF16),
            pltpu.VMEM((rows, 3 * width), BF16),
            pltpu.VMEM((PAIR, rows, width), BF16),
            pltpu.VMEM((nseq, n * crows, rows), BF16),
            pltpu.VMEM((rank3, n * crows), BF16),
            pltpu.VMEM((PAIR, model, 512), BF16),
            pltpu.VMEM((rows, model), BF16),
            pltpu.VMEM((rows, model), BF16),
            pltpu.VMEM((rows, model), BF16),
            pltpu.VMEM((rows, rank3 // 3), BF16),
            pltpu.VMEM((1, rank3 // 3, model), BF16),
            pltpu.VMEM((1, rank3 // 3, model), BF16),
            pltpu.VMEM((1, CORES * 2 * share, model), BF16),
            pltpu.VMEM((n * CORES * 2 * share, rows), BF16),
            dma((TRIPLE,)), dma((PAIR,)), dma((PAIR, 2)), dma((PAIR, 3)), dma((PAIR, 3)), dma((5,)), dma((5,)), dma((5,)), dma((5,)),
            dma((TRIPLE, nseq)), dma((TRIPLE, nseq)),
        ] + [dma((PAIR,))] * 8 + [dma((10,))] * 2 + [
            dma((PAIR,)), dma((PAIR,)), dma((PAIR,)), dma((nseq,)), dma((nseq,)), dma((nseq,)), dma((nseq,)), dma((nseq,)), dma((nseq,)),
            dma((PAIR, CORES * n + 2)), dma((1, 3, CORES * n)), dma((n,)), dma, dma((TRIPLE,)), dma((TRIPLE,)), dma((TRIPLE,)),
        ],
        compiler_params=pltpu.CompilerParams(collective_id=0, has_side_effects=True, vmem_limit_bytes=VMEM_LIMIT),
        cost_estimate=pl.CostEstimate(flops=flops, bytes_accessed=3 * x.size, transcendentals=nseq * rows * rows * width // dim),
        name="qkv_attention",
    )(x, gain, gain_mlp, wq, wk, wv, ar, agu, bqkv, wide, wo, wo_l, wo_r, wg, wu, wd, lml)


def kernel_b(n, keep, scale, rank, share,
             x, gain, att, wo, wo_l, wo_r, wo_f, wo_x, wide, wide_f, wide_x, agu, agu_oth, wg, wg_o, wu, wu_o, wd, wd_o, lml, lml_o,
             h_first, x1_first, mg_first,
             y, att_t,
             wob, gub, wdb, attv, xb, hb, mb, zb, zm, x1b, yb, in1l, in1r, in2l, in2r, in1m, in2ml, in2mr, mgu, aob, bob, agub, lgb, lub, adb, bdb, sel, mido, midg,
             wo_sem, gu_sem, wd_sem, att_sem, x_sem, lo_sem, lg_sem, bd_sem,
             s1r, s1l, s2r, s2l, ar, al, yown, fr, fl, r1l, r1r, r2l, r2r, gl, gr, hl, hr, dsend, drecv,
             t_rs, t_ls, t_rl, t_rr, t_frs, t_fls, t_fl, t_fr,
             z1s, z1r, z2rs, z2rr, z2ls, z2lr, m_send, m_recv, e_sem):
    core, chip, right, left, partner = ring(n)
    nseq, rows, model = att.shape[0], x.shape[1], x.shape[2]
    width = att.shape[3]
    ff = wg.shape[1]
    first = core * nseq
    late = nseq - keep
    crows = CORES * 2 * share
    blk = rows // n
    half = blk // 2
    before, after, opposite = lax.rem(chip + n - 1, n), lax.rem(chip + 1, n), lax.rem(chip + 2, n)
    beyond = opposite * CORES + core
    wo_t, gu_t, wd_t = wob.shape[2], gub.shape[3], wdb.shape[2]
    wo_n, gu_n, wd_n = model // wo_t, ff // gu_t, model // wd_t
    greet(right, left, partner, beyond)

    stage = OutStage(n, scale, rank, share, x, gain, (wo, wo_l, wo_r, wo_f, wo_x), (wide, wide_f, wide_x), (agu, agu_oth),
                     (wob, attv, xb, mido, aob, bob, agub), wo_sem, lo_sem)

    def gu_copies(k, own):
        at = pl.ds(pl.multiple_of(lax.rem(k, gu_n) * gu_t, gu_t), gu_t)
        slot = even(k)
        pair = (wg, wu) if own else (wg_o, wu_o)
        return [local(w.at[:, at], gub.at[slot, j], gu_sem.at[slot, j]) for j, w in enumerate(pair)]

    def gu_start(k):
        @pl.when(k < gu_n)
        def _():
            for c in gu_copies(k, True):
                c.start()

        @pl.when(k >= gu_n)
        def _():
            for c in gu_copies(k, False):
                c.start()

    def wd_copies(k):
        at = pl.ds(pl.multiple_of(k * wd_t, wd_t), wd_t)
        slot = even(k)
        return [local(w.at[:, at], wdb.at[slot, pl.ds(j * ff, ff)], wd_sem.at[slot, j]) for j, w in enumerate((wd, wd_o))]

    def att_copies(s):
        return [local(att.at[s, j], attv.at[:, pl.ds(j * width, width)], att_sem.at[j]) for j in range(n)]

    def att_start(s):
        @pl.when(s < keep)
        def _():
            start(att_copies(s))

        @pl.when(s >= keep)
        def _():
            k = jnp.maximum(s - keep, 0)
            late_in(k)
            for j, own in enumerate(att_copies(s)):
                @pl.when(chip == j)
                def _(own=own):
                    own.start()

                @pl.when(chip != j)
                def _(j=j):
                    local(att_t.at[k, j], attv.at[:, pl.ds(j * width, width)], att_sem.at[j]).start()

    def late_right(k):
        return remote(att.at[keep + k, chip], att_t.at[k, chip], t_rs.at[k], t_rl.at[k], right)

    def late_left(k):
        return remote(att.at[keep + k, chip], att_t.at[k, chip], t_ls.at[k], t_rr.at[k], left)

    def late_hops(k):
        a, b = att_t.at[k, before, head(rows // 2)], att_t.at[k, after, pl.ds(rows // 2, rows // 2)]
        return remote(a, a, t_frs.at[k], t_fl.at[k], right), remote(b, b, t_fls.at[k], t_fr.at[k], left)

    def late_pass(k):
        hop_r, hop_l = late_hops(k)
        remote(att.at[keep + k, chip], att_t.at[k, before], t_rs.at[k], t_rl.at[k], right).wait_recv()
        hop_r.start()
        remote(att.at[keep + k, chip], att_t.at[k, after], t_ls.at[k], t_rr.at[k], left).wait_recv()
        hop_l.start()

    def late_in(k):
        a, b = att_t.at[k, opposite, head(rows // 2)], att_t.at[k, opposite, pl.ds(rows // 2, rows // 2)]
        remote(a, a, t_frs.at[k], t_fl.at[k], right).wait_recv()
        remote(b, b, t_fls.at[k], t_fr.at[k], left).wait_recv()

    def x_copy(s):
        return local(x.at[first + s], xb, x_sem)

    def lora_o(s):
        return stage.lora(s, even(s))

    def lora_m(s):
        slot, out = even(s), []
        for j, (src, k) in enumerate(((lml, first + s), (lml_o, s))):
            at = pl.ds(j * ff, ff)
            out.append(local(src.at[k, head(rank)], lgb.at[slot, head(rank), at], lg_sem.at[slot, 3 * j]))
            out.append(local(src.at[k, pl.ds(rank, rank)], lub.at[slot, pl.ds(rank, rank), at], lg_sem.at[slot, 3 * j + 1]))
            out.append(local(src.at[k, pl.ds(2 * rank, rank)], adb.at[slot, head(rank), at], lg_sem.at[slot, 3 * j + 2]))
        return out

    def start(copies):
        for c in copies:
            c.start()

    def wait(copies):
        for c in copies:
            c.wait()

    def rows_of(j, size=blk, shift=0):
        return pl.ds(pl.multiple_of(j * blk + shift, size), size)

    def rs1_right(s):
        return remote(zb.at[third(s), rows_of(opposite, half)], in1l.at[third(s)], s1r.at[s], r1l.at[s], right)

    def rs1_left(s):
        return remote(zb.at[third(s), rows_of(opposite, half, half)], in1r.at[third(s)], s1l.at[s], r1r.at[s], left)

    def rs2_right(s):
        return remote(zb.at[third(s), rows_of(after)], in2l.at[third(s)], s2r.at[s], r2l.at[s], right)

    def rs2_left(s):
        return remote(zb.at[third(s), rows_of(before)], in2r.at[third(s)], s2l.at[s], r2r.at[s], left)

    def ag1_right(s):
        return remote(yb.at[even(s)], y.at[first + s, rows_of(chip)], ar.at[s], gl.at[s], right)

    def ag1_left(s):
        return remote(yb.at[even(s)], y.at[first + s, rows_of(chip)], al.at[s], gr.at[s], left)

    def ag1_own(s):
        return local(yb.at[even(s)], y.at[first + s, rows_of(chip)], yown.at[s])

    def ag2_right(s, block):
        part = y.at[first + s, rows_of(block, half)]
        return remote(part, part, fr.at[s], hl.at[s], right)

    def ag2_left(s, block):
        part = y.at[first + s, rows_of(block, half, half)]
        return remote(part, part, fl.at[s], hr.at[s], left)

    def across(s, k, block):
        part = y.at[first + s, rows_of(block)]
        return remote(yb.at[even(s)] if k == 0 else part, part, dsend.at[k, s], drecv.at[k, s], partner)

    def across_in(s, k):
        there = y.at[(1 - core) * nseq + s, rows_of((chip, before, after, opposite)[k])]
        return remote(there, there, dsend.at[k, s], drecv.at[k, s], partner)

    def lanes_of(j):
        return pl.ds(pl.multiple_of(j * blk, blk), blk)

    def zm1(s):
        return remote(zm.at[third(s), :, lanes_of(opposite)], in1m.at[third(s)], z1s.at[s], z1r.at[s], right)

    def zm2_right(s):
        return remote(zm.at[third(s), :, lanes_of(after)], in2ml.at[third(s)], z2rs.at[s], z2rr.at[s], right)

    def zm2_left(s):
        return remote(zm.at[third(s), :, lanes_of(before)], in2mr.at[third(s)], z2ls.at[s], z2lr.at[s], left)

    def rank_rows(j):
        return pl.ds(pl.multiple_of(j * crows, crows), crows)

    def mid_copies(s, froms):
        return [remote(mgu.at[s, rank_rows(j)], mgu.at[s, rank_rows(j)], m_send.at[k, s], m_recv.at[k, s], to)
                for k, (j, to) in enumerate(zip(froms, (right, left, beyond)))]

    def do_rs2(s):
        slot = third(s)
        zm1(s).wait_recv()
        at = lanes_of(after)
        zm[slot, :, at] = (zm[slot, :, at].astype(F32) + in1m[slot].astype(F32)).astype(BF16)
        zm2_right(s).start()
        zm2_left(s).start()
        rs1_right(s).wait_recv()
        at = rows_of(after, half)
        zb[slot, at, :] = (zb[slot, at, :].astype(F32) + in1l[slot].astype(F32)).astype(BF16)
        rs2_right(s).start()
        rs1_left(s).wait_recv()
        at = rows_of(before, half, half)
        zb[slot, at, :] = (zb[slot, at, :].astype(F32) + in1r[slot].astype(F32)).astype(BF16)
        rs2_left(s).start()

    def do_rs3(s):
        slot, yslot = third(s), even(s)

        @pl.when(s >= 2)
        def _():
            ag1_right(s - 2).wait_send()
            ag1_left(s - 2).wait_send()
            ag1_own(s - 2).wait()
            across(s - 2, 0, chip).wait_send()

        rs2_right(s).wait_recv()
        rs2_left(s).wait_recv()
        mine = zb.at[slot, rows_of(chip)]
        zm2_right(s).wait_recv()
        zm2_left(s).wait_recv()
        mid = zm[slot, :, lanes_of(chip)].astype(F32) + in2ml[slot].astype(F32) + in2mr[slot].astype(F32)
        mid = mid.T.astype(BF16)

        def piece(k, carry):
            at = pl.ds(pl.multiple_of(k * wo_t, wo_t), wo_t)
            z = mine[:, at].astype(F32) + in2l[slot, :, at].astype(F32) + in2r[slot, :, at].astype(F32)
            z = z + scale * dot(mid, bdb[s, :, at])
            yb[yslot, :, at] = (x1b[lax.rem(s, 4), :, at].astype(F32) + z).astype(BF16)
            return carry

        loop(wo_n, piece, 0)
        ag1_right(s).start()
        ag1_left(s).start()
        ag1_own(s).start()
        across(s, 0, chip).start()

    def do_ag2(s):
        remote(yb.at[0], y.at[first + s, rows_of(before)], ar.at[s], gl.at[s], right).wait_recv()
        ag2_right(s, before).start()
        across(s, 1, before).start()
        remote(yb.at[0], y.at[first + s, rows_of(after)], al.at[s], gr.at[s], left).wait_recv()
        ag2_left(s, after).start()
        across(s, 2, after).start()

    def do_across(s):
        ag2_right(s, opposite).wait_recv()
        ag2_left(s, opposite).wait_recv()
        across(s, 3, opposite).start()

    def when(cond, f, s):
        @pl.when(cond)
        def _():
            f(s)

    for k in range(min(late, 2)):
        late_right(k).start()
        late_left(k).start()
    bd_copies = [local(stage.share_of((wide, wide_f, wide_x), cross, j).at[pl.ds(0 if cross else first, nseq), pl.ds(2 * rank, rank)],
                       bdb.at[:, :, stage.cols(d)], bd_sem.at[4 * cross + j]) for d, cross, j in stage.shares]
    done = [local(h_first, hb.at[0], e_sem.at[0]), local(x1_first, x1b.at[0], e_sem.at[1]), local(mg_first, mgu.at[0], e_sem.at[2])]
    start(done)
    start(bd_copies)
    sel[...] = pick(sel.shape, share, rank, 2, 1)
    for k in range(2):
        start(stage.wo_copies(k))
        start(gu_copies(k, True))
        start(wd_copies(k))
    att_start(jnp.int32(1))
    x_copy(1).start()
    start(lora_o(1))
    lgb[...] = jnp.zeros_like(lgb)
    lub[...] = jnp.zeros_like(lub)
    start(lora_m(0))
    wait(bd_copies)
    wait(done)

    def out_proj(s):
        slot = even(s)
        wait(lora_o(s))
        wait(att_copies(s))
        x_copy(s).wait()
        stage.first_product(slot)
        stage.tiles(slot, 0, wo_n // 2, s + 1 < nseq)

    def out_proj_end(s):
        slot = even(s)
        stage.tiles(slot, wo_n // 2, wo_n, s + 1 < nseq)
        stage.norm(slot, hb.at[slot], mgu.at[s, rank_rows(chip)])
        start(mid_copies(s, (chip, chip, chip)))
        for k in range(2, late):
            @pl.when(s == k - 1)
            def _(k=k):
                late_right(k).start()
                late_left(k).start()

        x1b[lax.rem(s, 4)] = xb[rows_of(chip), :]

        @pl.when(s + 1 < nseq)
        def _():
            start(lora_o(s + 1))
            att_start(s + 1)
            x_copy(s + 1).start()

    def gate_up(s):
        slot = even(s)
        @pl.when(s >= 1)
        def _():
            for c in mid_copies(s, (before, after, opposite)):
                c.wait_recv()

        midg[...] = dot(sel[...], mgu[s]).T.astype(BF16)
        wait(lora_m(s))
        gate_tiles(s, 0, gu_n)

    def gate_tiles(s, lo, hi):
        slot = even(s)
        h = hb.at[slot]
        mid = midg[...]

        def tile(k, carry):
            at = pl.ds(pl.multiple_of(k * gu_t, gu_t), gu_t)
            wait(gu_copies(k, True))
            g = dot(h[...], gub[even(k), 0]) + scale * dot(mid, lgb[slot, :, at])
            u = dot(h[...], gub[even(k), 1]) + scale * dot(mid, lub[slot, :, at])
            g = g.astype(BF16).astype(F32)
            u = u.astype(BF16).astype(F32)
            mb[:, at] = (jax.nn.silu(g) * u).astype(BF16)

            @pl.when((k + 2 < 2 * gu_n) | (s + 1 < nseq))
            def _():
                gu_start(lax.rem(k + 2, 2 * gu_n))

            return carry

        lax.fori_loop(lo, hi, tile, 0)

    def gate_up_end(s):
        gate_tiles(s, gu_n, 2 * gu_n)

        @pl.when(s + 1 < nseq)
        def _():
            start(lora_m(s + 1))

    def down(s):
        slot = third(s)

        @pl.when(s >= 3)
        def _():
            rs1_right(s - 3).wait_send()
            rs1_left(s - 3).wait_send()
            rs2_right(s - 3).wait_send()
            rs2_left(s - 3).wait_send()
            zm1(s - 3).wait_send()
            zm2_right(s - 3).wait_send()
            zm2_left(s - 3).wait_send()

        zm[slot] = dot_nt(adb[even(s)], mb[...]).astype(BF16)

        def tile(k, carry):
            at = pl.ds(pl.multiple_of(k * wd_t, wd_t), wd_t)
            wait(wd_copies(k))
            zb[slot, :, at] = dot(mb[...], wdb[even(k)]).astype(BF16)

            @pl.when((k + 2 < wd_n) | (s + 1 < nseq))
            def _():
                start(wd_copies(lax.rem(k + 2, wd_n)))

            return carry

        loop(wd_n, tile, 0)
        zm1(s).start()
        rs1_right(s).start()
        rs1_left(s).start()

    def step(f, t, lag, ahead=0):
        s = t - lag + ahead
        when((s >= 0) & (s < nseq), f, s)

    def body(t, carry):
        step(out_proj, t, 0, 1)
        step(do_rs3, t, 2)
        step(out_proj_end, t, 0, 1)
        for k, stages in enumerate(((), (gate_up, do_rs2, do_ag2, gate_up_end), (down,))):
            for f in stages:
                step(f, t, {do_rs2: 1, do_ag2: 2}.get(f, 0))
            if k < late:
                when(t == 0, lambda _, k=k: late_pass(k), t)
        step(do_across, t, 3)
        return carry

    loop(nseq + 3, body, 0)

    for s in range(max(nseq - 3, 0), nseq):
        rs1_right(s).wait_send()
        rs1_left(s).wait_send()
        rs2_right(s).wait_send()
        rs2_left(s).wait_send()
        zm1(s).wait_send()
        zm2_right(s).wait_send()
        zm2_left(s).wait_send()
    for s in range(max(nseq - 2, 0), nseq):
        ag1_right(s).wait_send()
        ag1_left(s).wait_send()
        ag1_own(s).wait()
        across(s, 0, chip).wait_send()

    def finish(s, carry):
        @pl.when(s >= 1)
        def _():
            for c in mid_copies(s, (chip, chip, chip)):
                c.wait_send()

        ag2_right(s, before).wait_send()
        ag2_left(s, after).wait_send()
        for k, block in ((1, before), (2, after), (3, opposite)):
            across(s, k, block).wait_send()
        for k in range(4):
            across_in(s, k).wait_recv()
        return carry

    loop(nseq, finish, 0)
    for k in range(late):
        late_right(k).wait_send()
        late_left(k).wait_send()
        for hop in late_hops(k):
            hop.wait_send()


def call_b(n, keep, scale, rank, share, x, gain, att, wo, wo_l, wo_r, wo_f, wo_x, wide, wide_f, wide_x, agu, agu_oth, wg, wg_o, wu, wu_o, wd, wd_o, lml, lml_o, h_first, x1_first, mg_first):
    nseq, rows, model, ff = att.shape[0], x.shape[1], x.shape[2], wg.shape[1]
    hbm = pl.BlockSpec(memory_space=pl.ANY)
    vmem = pl.BlockSpec(memory_space=pltpu.VMEM)
    dma = pltpu.SemaphoreType.DMA
    blk = rows // n
    ndev = CORES * n
    tile = 512
    flops = 2 * nseq * rows * (model * model + 3 * model * ff * CORES)
    return pl.pallas_call(
        functools.partial(kernel_b, n, keep, scale, rank, share),
        out_shape=[jax.ShapeDtypeStruct(x.shape, BF16), jax.ShapeDtypeStruct((nseq - keep, *att.shape[1:]), BF16)],
        in_specs=[hbm, vmem] + [hbm] * 22,
        out_specs=[hbm] * 2,
        scratch_shapes=[
            pltpu.VMEM((PAIR, model, tile), BF16),
            pltpu.VMEM((PAIR, 2, model, tile // 2), BF16),
            pltpu.VMEM((PAIR, CORES * ff, tile), BF16),
            pltpu.VMEM((rows, model), BF16),
            pltpu.VMEM((rows, model), BF16),
            pltpu.VMEM((PAIR, rows, model), BF16),
            pltpu.VMEM((rows, CORES * ff), BF16),
            pltpu.VMEM((TRIPLE, rows, model), BF16),
            pltpu.VMEM((TRIPLE, rank, rows), BF16),
            pltpu.VMEM((QUAD, blk, model), BF16),
            pltpu.VMEM((PAIR, blk, model), BF16),
            pltpu.VMEM((TRIPLE, blk // 2, model), BF16),
            pltpu.VMEM((TRIPLE, blk // 2, model), BF16),
            pltpu.VMEM((TRIPLE, blk, model), BF16),
            pltpu.VMEM((TRIPLE, blk, model), BF16),
            pltpu.VMEM((TRIPLE, rank, blk), BF16),
            pltpu.VMEM((TRIPLE, rank, blk), BF16),
            pltpu.VMEM((TRIPLE, rank, blk), BF16),
            pltpu.VMEM((nseq, n * CORES * 2 * share, rows), BF16),
            pltpu.VMEM((PAIR, rank, model), BF16),
            pltpu.VMEM((PAIR, rank, model), BF16),
            pltpu.VMEM((PAIR, CORES * 2 * share, model), BF16),
            pltpu.VMEM((PAIR, 2 * rank, CORES * ff), BF16),
            pltpu.VMEM((PAIR, 2 * rank, CORES * ff), BF16),
            pltpu.VMEM((PAIR, rank, CORES * ff), BF16),
            pltpu.VMEM((nseq, rank, model), BF16),
            pltpu.VMEM((2 * rank, 2 * rank), BF16),
            pltpu.VMEM((rows, rank), BF16),
            pltpu.VMEM((rows, 2 * rank), BF16),
            dma((PAIR, ndev + 2)), dma((PAIR, 2)), dma((PAIR, 2)), dma((n,)), dma, dma((PAIR, 3, ndev)), dma((PAIR, 6)), dma((ndev,)),
        ] + [dma((nseq,))] * 17 + [dma((QUAD, nseq))] * 2 + [dma((nseq - keep,))] * 8 + [dma((nseq,))] * 6 + [dma((TRIPLE, nseq))] * 2 + [dma((TRIPLE,))],
        compiler_params=pltpu.CompilerParams(collective_id=1, has_side_effects=True, vmem_limit_bytes=VMEM_LIMIT),
        cost_estimate=pl.CostEstimate(flops=flops, bytes_accessed=4 * x.size, transcendentals=0),
        name="out_mlp",
    )(x, gain, att, wo, wo_l, wo_r, wo_f, wo_x, wide, wide_f, wide_x, agu, agu_oth, wg, wg_o, wu, wu_o, wd, wd_o, lml, lml_o, h_first, x1_first, mg_first)[0]


def solution(mesh):
    n = mesh.shape["tp"] // CORES
    act_spec = P("dp", N, N)
    w_head, w_out, w_col, w_row = P(N, "tp", N), P("tp", N, N), P(N, "tp"), P("tp", N)
    a_rank, b_head, b_col = P(N, N, "tp"), P(N, N, "tp", N), P(N, N, "tp")
    a_head, a_row = P(N, "tp", N, N), P(N, "tp", N)
    in_specs = (act_spec, P("dp"), P(N), P(N), w_head, w_head, w_head, w_out, w_col, w_col, w_row,
                a_rank, b_head, a_rank, b_head, a_rank, b_head, a_head, b_col, a_rank, b_col, a_rank, b_col, a_row, b_col)

    def local_layer(x_in, adapter_ids, gain_attn, gain_mlp, w_q, w_k, w_v, w_o, w_gate, w_up, w_down,
                    a_q, b_q, a_k, b_k, a_v, b_v, a_o, b_o, a_gate, b_gate, a_up, b_up, a_down, b_down):
        nseq, model = x_in.shape[0], x_in.shape[2]
        rank, dim = b_q.shape[1], w_q.shape[2]
        own = w_q.shape[1] * dim
        scale = LORA_ALPHA / rank
        share = a_q.shape[2]
        group = math.lcm(dim, 128) // dim
        keep = max(nseq // CORES - 3, 1)

        def take(*stacks):
            return jnp.take(jnp.concatenate(stacks, axis=1), adapter_ids, axis=0, mode="clip")

        def turn(stack):
            return jnp.swapaxes(stack, 1, 2)

        wo = w_o.reshape(own, model)
        ndev = n * CORES
        upper = wo[:own // 2]
        wo_l = lax.ppermute(upper, "tp", [(d, (d + CORES) % ndev) for d in range(ndev)])
        wo_r = lax.ppermute(upper, "tp", [((d + CORES) % ndev, d) for d in range(ndev)])
        ar = take(turn(a_q), turn(a_k), turn(a_v), jnp.zeros((a_q.shape[0], share, model), BF16))
        agu = take(turn(a_gate), turn(a_up))
        bqkv = take(*[b.reshape(-1, rank, own) for b in (b_q, b_k, b_v)])
        wide = take(turn(a_o.reshape(-1, own, rank)), b_o, b_down)
        lml = take(b_gate, b_up, turn(a_down))
        flat = [jnp.transpose(w, (1, 2, 0)).reshape(own, model) for w in (w_q, w_k, w_v)]
        att, _, agu_oth, _, wide_f, wide_x, wo_f, wo_x, wg_o, wu_o, wd_o, lml_o, *head = call_a(
            n, keep, scale, group, dim, share, x_in, gain_attn.reshape(1, model), gain_mlp.reshape(1, model), *flat, ar, agu, bqkv, wide,
            wo, wo_l, wo_r, w_gate, w_up, w_down, lml)
        return call_b(n, keep, scale, rank, share, x_in, gain_mlp.reshape(1, model), att, wo, wo_l, wo_r, wo_f, wo_x, wide, wide_f, wide_x,
                      agu, agu_oth, w_gate, wg_o, w_up, wu_o, w_down, wd_o, lml, lml_o, *head)

    return jax.shard_map(local_layer, mesh=mesh, in_specs=in_specs, out_specs=act_spec, check_vma=False)
```

time: 858 us -> 805 us (0.938)
  Pallas kernels: 806 us -> 737 us
  waiting for transfers between devices: 0 us -> 13.4 us
    pallas_call x1, Pallas kernels: 309 us -> 235 us  [call_a(): pl.pallas_call(functools.partial(kernel_a, n, lag, keep, scale, group, di...]
    ppermute x0 -> x2, waiting for transfers between devices: none -> 13.4 us  [the longest x1 10.1 us: local_layer(): lax.ppermute(upper, 'tp', [((d + CORES) % ndev, d) for d in range(ndev)])]
    unnamed x18 -> x26, local copies, waits for them, and re-layouts: 33.6 us -> 33.7 us
  transfers between devices with their start and end apart: 0 -> 2, of which waited for: 0 -> 2; matrix products, arithmetic and copies ran while one was open for 0% -> 2% of each run, Pallas kernels for 0% -> 0%
where the time goes in v2:
time: 805 us
  Pallas kernels  737 us (92%)
  local copies, waits for them, and re-layouts  46.9 us (6%)
  waiting for transfers between devices  13.4 us (2%)
    pallas_call x1, Pallas kernels, call_b(): pl.pallas_call(functools.partial(kernel_b, n, keep, scale, rank, share),...  502 us
    pallas_call x1, Pallas kernels, call_a(): pl.pallas_call(functools.partial(kernel_a, n, lag, keep, scale, group, di...  235 us
    unnamed x26, local copies, waits for them, and re-layouts  33.7 us
  transfers between devices with their start and end apart: 2, of which 2 were waited for; matrix products, arithmetic and copies ran while one was open for 2% of the time, Pallas kernels for 0%

profile of v2, /device:TPU:113, one launch (start us, length us, event | category | flops | bytes accessed | tf_op | source)
XLA Modules:
  0.0 804.7 jit_solution(5931173579009740656)
XLA Ops:
  0.0 2.5 slice.6
  2.6 3.7 collective-permute-start.1
  6.3 0.4 reshape.37
  6.7 0.4 reshape.38
  7.1 0.4 reshape.39
  7.4 0.3 copy.26
  7.7 0.4 reshape.40
  8.1 0.0 copy-start.4
  8.1 0.1 pad_maximum_fusion.1
  8.2 1.7 gather_fusion.2
  10.0 0.1 pad_maximum_fusion.2
  10.1 1.7 gather_fusion.3
  11.8 0.4 pad_maximum_fusion.3
  12.2 1.5 gather_fusion.1
  13.7 0.1 pad.14.clone
  13.8 0.8 maximum_maximum_fusion
  14.6 1.8 gather_fusion
  16.4 2.0 pad_maximum_fusion
  18.5 2.4 gather_fusion.4
  20.9 10.1 %collective-permute-done.1.wo_r = bf16[192,3072]{1,0:T(8,128)(2,1)} collective-permute-done((bf16[192,3072]{1,0:T(8,128)(2,1)}, bf16[192,3072]{1,0:T(8,128)(2,1)}, u32[]{:S(2)}, u32[]{:S(2)}) %collective-permute-start.1) | collective-permute-done | bytes 1179680 | tf_op jit(solution)/shard_map/ppermute | solution.py:1107
  31.0 3.3 collective-permute-done.wo_l
  34.2 235.1 %qkv_attention.1 = (bf16[8,4,512,768]{3,2,1,0:T(8,128)(2,1)}, bf16[8,16,3072]{2,1,0:T(8,128)(2,1)}, bf16[8,8,3072]{2,1,0:T(8,128)(2,1)}, bf16[8,96,384]{2,1,0:T(...) custom-call(bf16[16,512,3072]{2,1,0:T(8,128)(2,1)} %x.3, ...), custom_call_target="tpu_custom_call" | custom-call | flops 60397977600 | bytes 75497472 | tf_op jit(solution)/shard_map/qkv_attention/pallas_call | solution.py:561
  269.3 502.0 %out_mlp.1 = (bf16[16,512,3072]{2,1,0:T(8,128)(2,1)}, bf16[3,4,512,768]{3,2,1,0:T(8,128)(2,1)}) custom-call(bf16[16,512,3072]{2,1,0:T(8,128)(2,1)} %x.3, f32[1,3072]{1,0:T(1,128)} %bitcast.36, bf16[8,4,512,768]{3,2,1,0:T(8,128)(2,1)} %get-tuple-element.19.att, bf16[384,3072]{1,0:T(8,128)(2,1)} %bitcast.25, bf16[192,3072]{1,0:T(8,128)(2,1)} %collective-permute-done.wo_l, ...), custom_call_target="tpu_custom_call" | custom-call | flops 231928233984 | bytes 100663296 | tf_op jit(solution)/shard_map/out_mlp/pallas_call | solution.py:1035
  771.4 33.3 %copy.28 = bf16[16,512,3072]{2,1,0:T(8,128)(2,1)} copy(bf16[16,512,3072]{2,1,0:T(8,128)(2,1)} %get-tuple-element.32) | data formatting | bytes 100663296
  (26 shorter events, 0.1 us)
Async XLA Ops:
  0.0 6.3 copy-start.11
  0.0 6.3 copy-start
  0.0 6.7 copy-start.1
  0.0 7.0 copy-start.2
  0.0 7.4 copy-start.3
  2.6 28.4 %collective-permute-start.1 = (bf16[192,3072]{1,0:T(8,128)(2,1)}, bf16[192,3072]{1,0:T(8,128)(2,1)}, u32[]{:S(2)}, u32[]{:S(2)}) collective-permute-start(bf16[192,3072]{1,0:T(8,128)(2,1)} %bitcast.15), channel_id=1, source_target_pairs={{2,0},{3,1},{4,2},{5,3},{6,4},{7,5},{0,6},{1,7},{10,8},{11,9},{12,... | collective-permute-start | bytes 3538952 | tf_op jit(solution)/shard_map/ppermute | solution.py:1107
  6.3 28.0 %collective-permute-start = (bf16[192,3072]{1,0:T(8,128)(2,1)}, bf16[192,3072]{1,0:T(8,128)(2,1)}, u32[]{:S(2)}, u32[]{:S(2)}) collective-permute-start(bf16[192,3072]{1,0:T(8,128)(2,1)} %bitcast.15), channel_id=1, source_target_pairs={{0,2},{1,3},{2,4},{3,5},{4,6},{5,7},{6,0},{7,1},{8,10},{9,11},{10,... | collective-permute-start | bytes 3538952 | tf_op jit(solution)/shard_map/ppermute | solution.py:1106
  8.1 1.9 copy-start.4
  8.1 1.9 copy-start.5
  10.0 1.9 copy-start.6
  10.0 1.9 copy-start.7
  10.1 3.7 copy-start.8
  10.1 3.7 copy-start.9
  11.8 2.0 copy-start.10

commit v3 on v2

--- a/solution.py
+++ b/solution.py
@@ -140,8 +140,8 @@
         self.wide_refs, self.agu_refs, self.bufs = wide_refs, agu_refs, bufs
         self.wo_sem, self.lo_sem = wo_sem, lo_sem
         self.rows, self.first = x.shape[1], self.core * (x.shape[0] // CORES)
-        wo, wo_l, wo_r, wo_f, wo_x = wo_refs
-        hi, deep = wo_l.shape[0], wo.shape[0]
+        wo, wo_p, wo_f, wo_x = wo_refs
+        deep = wo.shape[0]
         self.width = wide_refs[0].shape[2]
         self.tile_w = bufs[0].shape[2]
         self.tiles_n = x.shape[2] // self.tile_w
@@ -150,12 +150,10 @@
         self.shares += [(CORES * c + 1 - self.core, 1, j) for j, c in enumerate(chips)]
         self.wo_shares = []
         for d, cross, j in self.shares:
-            base = pl.multiple_of(d * deep, deep)
-            if cross or j in (0, 3):
-                self.wo_shares.append((self.share_of((wo, wo_f, wo_x), cross, j), pl.ds(base, deep)))
-            else:
-                self.wo_shares.append(((wo_l, wo_r)[j - 1], pl.ds(base, hi)))
-                self.wo_shares.append((wo_f.at[j - 1, pl.ds(hi, deep - hi)], pl.ds(base + hi, deep - hi)))
+            src = self.share_of((wo, wo_f, wo_x), cross, j)
+            early = wo_p if not cross and j in (1, 2) else src
+            both = (early, src) if j == 1 else (src, early)
+            self.wo_shares.append((both, pl.ds(pl.multiple_of(d * deep, deep), deep)))
 
     @staticmethod
     def share_of(refs, cross, j):
@@ -164,11 +162,18 @@
     def cols(self, d):
         return pl.ds(pl.multiple_of(d * self.width, self.width), self.width)
 
-    def wo_copies(self, k):
+    def wo_copies(self, k, core=0):
         wob = self.bufs[0]
         at, slot = pl.ds(pl.multiple_of(k * self.tile_w, self.tile_w), self.tile_w), even(k)
-        return [local(src.at[:, at], wob.at[slot, rows_at], self.wo_sem.at[slot, j])
-                for j, (src, rows_at) in enumerate(self.wo_shares)]
+        return [local(both[core].at[:, at], wob.at[slot, rows_at], self.wo_sem.at[slot, j])
+                for j, (both, rows_at) in enumerate(self.wo_shares)]
+
+    def wo_start(self, k):
+        for core in range(CORES):
+            @pl.when(self.core == core)
+            def _(core=core):
+                for c in self.wo_copies(k, core):
+                    c.start()
 
     def lora(self, s, slot):
         _, _, _, _, aob, bob, agub = self.bufs
@@ -199,8 +204,7 @@
 
             @pl.when((k + 2 < self.tiles_n) | more)
             def _():
-                for c in self.wo_copies(lax.rem(k + 2, self.tiles_n)):
-                    c.start()
+                self.wo_start(lax.rem(k + 2, self.tiles_n))
 
             return carry
 
@@ -213,7 +217,7 @@
 
 
 def kernel_a(n, lag, keep, scale, group, dim, share,
-             x, gain, gain_mlp, wq, wk, wv, ar, agu, bqkv, wide, wo, wo_l, wo_r, wg, wu, wd, lml,
+             x, gain, gain_mlp, wq, wk, wv, ar, agu, bqkv, wide, wo, wo_p, wg, wu, wd, lml,
              att, ar_oth, agu_oth, b_oth, wide_f, wide_x, wo_f, wo_x, wg_o, wu_o, wd_o, lml_o, h_out, x1_out, mg_out,
              wbuf, xbuf, hbuf, abuf, bbuf, qkv, attb, mids, sel, wob, attv, xb, hb, mido, aob, bob, agub, mgu,
              w_sem, x_sem, a_sem, bo_sem, bp_sem, d_send, d_recv, o_send, o_recv, m_send, m_recv,
@@ -241,70 +245,80 @@
                                      (agu.at[theirs], agu_oth)))]
     mine = [local(w, wbuf.at[pl.ds(p * width + core * own, own)], w_sem.at[p]) for p, w in enumerate((wq, wk, wv))]
 
-    hi = wo_l.shape[0]
-    whole, top, low = head(wo.shape[0]), head(hi), pl.ds(hi, wo.shape[0] - hi)
-    wide_half = wide.shape[0] // 2
     to_right, to_left = (right, pr_send, prl_recv, pfr_send, pfl_recv), (left, pl_send, prr_recv, pfl_send, pfr_recv)
+
+    def by_core(f):
+        for c in range(CORES):
+            @pl.when(core == c)
+            def _(c=c):
+                f(c)
 
     def pack_first(k, way):
         to, send, recv, _, _ = (to_right, to_left)[way]
-        if k == 0:
-            return remote(wide, wide_f.at[way], send.at[k], recv.at[k], to)
-        return remote(wo.at[low], wo_f.at[way, low], send.at[k], recv.at[k], to)
-
-    def pack_second(k, way):
+        src, dst = ((wide, wide_f), (wo, wo_f))[k]
+        return remote(src, dst.at[way], send.at[k], recv.at[k], to)
+
+    def pack_second(k, way, early=False):
         to, _, _, send, recv = (to_right, to_left)[way]
-        if k == 0:
-            part = pl.ds(way * wide_half, wide_half)
-            return remote(wide_f.at[way, part], wide_f.at[2, part], send.at[k], recv.at[k], to)
-        part = (top, low)[way]
-        return remote(wo_l if way == 0 else wo_f.at[1, low], wo_f.at[2, part], send.at[k], recv.at[k], to)
+        dst = (wide_f, wo_f)[k]
+        part_n = dst.shape[1] // 2
+        part = pl.ds(way * part_n, part_n)
+        return remote(wo_p.at[part] if early else dst.at[way, part], dst.at[2, part], send.at[k], recv.at[k], to)
 
     def wide_push(j):
         src = wide if j == 0 else wide_f.at[j - 1]
         return remote(src.at[theirs], wide_x.at[j], pp_send.at[j], pp_recv.at[j], partner)
 
-    def wo_push(j):
-        src, dst = ((wo, wo_x.at[0]), (wo_l, wo_x.at[1, top]), (wo_r, wo_x.at[2, top]), (wo_f.at[0, low], wo_x.at[1, low]),
-                    (wo_f.at[1, low], wo_x.at[2, low]), (wo_f.at[2], wo_x.at[3]))[j]
-        return remote(src, dst, pp_send.at[4 + j], pp_recv.at[4 + j], partner)
+    def wo_push(j, early=False):
+        src = wo if j == 0 else wo_p if early else wo_f.at[j - 1]
+        return remote(src, wo_x.at[j], pp_send.at[QUAD + j], pp_recv.at[QUAD + j], partner)
+
+    def wo_first(c):
+        pack_first(1, 1 - c).start()
+        wo_push(0).start()
+        wo_push(1 + c, True).start()
+
+    def wo_next(c):
+        pack_first(1, 1 - c).wait_recv()
+        pack_second(1, 1 - c).start()
+        wo_push(2 - c).start()
 
     def pack_start(k):
-        for way in range(2):
+        if k == 1:
+            by_core(wo_first)
+            return
+        for way in range(PAIR):
             pack_first(k, way).start()
-        if k == 0:
-            wide_push(0).start()
-        else:
-            for j in range(3):
-                wo_push(j).start()
+        wide_push(0).start()
 
     def pack_pass(k):
-        for way in range(2):
+        if k == 1:
+            by_core(wo_next)
+            return
+        for way in range(PAIR):
             pack_first(k, way).wait_recv()
-            if k == 0 or way == 1:
-                pack_second(k, way).start()
-            (wide_push(way + 1) if k == 0 else wo_push(way + 3)).start()
+            pack_second(k, way).start()
+            wide_push(way + 1).start()
 
     def pack_across(k):
-        for way in range(2):
+        for way in range(PAIR):
             pack_second(k, way).wait_recv()
-        (wide_push(3) if k == 0 else wo_push(5)).start()
+        (wide_push if k == 0 else wo_push)(TRIPLE).start()
 
     def wo_ready():
-        for j in range(4):
+        for j in range(QUAD):
             wide_push(j).wait_recv()
-        for j in range(6):
             wo_push(j).wait_recv()
-        far[4].wait_recv()
+        far[QUAD].wait_recv()
 
     def pack_end():
-        for k in range(2):
-            for way in range(2):
-                pack_first(k, way).wait_send()
+        for way in range(PAIR):
+            pack_first(0, way).wait_send()
+            for k in range(PAIR):
                 pack_second(k, way).wait_send()
-        for j in range(4):
+        by_core(lambda c: pack_first(1, 1 - c).wait_send())
+        for j in range(QUAD):
             wide_push(j).wait_send()
-        for j in range(6):
             wo_push(j).wait_send()
 
     def x_copy(g):
@@ -369,7 +383,7 @@
         return carry
 
     loop(nseq, first_product, 0)
-    pack_second(1, 0).start()
+    by_core(lambda c: pack_second(1, c, True).start())
     for c in near[1:]:
         c.wait()
     for c in b_copies(0):
@@ -430,14 +444,16 @@
                 local(xb.at[pl.ds(pl.multiple_of(chip * blk, blk), blk)], x1_out, e_sem.at[1])]
 
     def first_out():
-        stage = OutStage(n, scale, rank, share, x, gain_mlp, (wo, wo_l, wo_r, wo_f, wo_x), (wide, wide_f, wide_x),
+        stage = OutStage(n, scale, rank, share, x, gain_mlp, (wo, wo_p, wo_f, wo_x), (wide, wide_f, wide_x),
                          (agu, agu_oth), (wob, attv, xb, mido, aob, bob, agub), wo_sem, lo_sem)
         wo_ready()
         gathered(0)
         loads = [local(att.at[0, j], attv.at[:, pl.ds(j * width, width)], att_sem.at[j]) for j in range(n)]
         loads += [local(x.at[first], xb, xo_sem)] + stage.lora(0, 0)
-        for c in loads + stage.wo_copies(0) + stage.wo_copies(1):
+        for c in loads:
             c.start()
+        for k in range(PAIR):
+            stage.wo_start(k)
         for c in loads:
             c.wait()
         stage.first_product(0)
@@ -547,7 +563,7 @@
         c.wait()
 
 
-def call_a(n, keep, scale, group, dim, share, x, gain, gain_mlp, wq, wk, wv, ar, agu, bqkv, wide, wo, wo_l, wo_r, wg, wu, wd, lml):
+def call_a(n, keep, scale, group, dim, share, x, gain, gain_mlp, wq, wk, wv, ar, agu, bqkv, wide, wo, wo_p, wg, wu, wd, lml):
     nseq, rows, model = x.shape[0] // CORES, x.shape[1], x.shape[2]
     own = wq.shape[0]
     width = own * CORES
@@ -577,7 +593,7 @@
             jax.ShapeDtypeStruct((rows // n, model), BF16),
             jax.ShapeDtypeStruct((n * CORES * 2 * share, rows), BF16),
         ],
-        in_specs=[hbm, vmem, vmem] + [hbm] * 14,
+        in_specs=[hbm, vmem, vmem] + [hbm] * 13,
         out_specs=[hbm] * 15,
         scratch_shapes=[
             pltpu.VMEM((3 * width, model), BF16),
@@ -607,11 +623,11 @@
         compiler_params=pltpu.CompilerParams(collective_id=0, has_side_effects=True, vmem_limit_bytes=VMEM_LIMIT),
         cost_estimate=pl.CostEstimate(flops=flops, bytes_accessed=3 * x.size, transcendentals=nseq * rows * rows * width // dim),
         name="qkv_attention",
-    )(x, gain, gain_mlp, wq, wk, wv, ar, agu, bqkv, wide, wo, wo_l, wo_r, wg, wu, wd, lml)
+    )(x, gain, gain_mlp, wq, wk, wv, ar, agu, bqkv, wide, wo, wo_p, wg, wu, wd, lml)
 
 
 def kernel_b(n, keep, scale, rank, share,
-             x, gain, att, wo, wo_l, wo_r, wo_f, wo_x, wide, wide_f, wide_x, agu, agu_oth, wg, wg_o, wu, wu_o, wd, wd_o, lml, lml_o,
+             x, gain, att, wo, wo_p, wo_f, wo_x, wide, wide_f, wide_x, agu, agu_oth, wg, wg_o, wu, wu_o, wd, wd_o, lml, lml_o,
              h_first, x1_first, mg_first,
              y, att_t,
              wob, gub, wdb, attv, xb, hb, mb, zb, zm, x1b, yb, in1l, in1r, in2l, in2r, in1m, in2ml, in2mr, mgu, aob, bob, agub, lgb, lub, adb, bdb, sel, mido, midg,
@@ -634,7 +650,7 @@
     wo_n, gu_n, wd_n = model // wo_t, ff // gu_t, model // wd_t
     greet(right, left, partner, beyond)
 
-    stage = OutStage(n, scale, rank, share, x, gain, (wo, wo_l, wo_r, wo_f, wo_x), (wide, wide_f, wide_x), (agu, agu_oth),
+    stage = OutStage(n, scale, rank, share, x, gain, (wo, wo_p, wo_f, wo_x), (wide, wide_f, wide_x), (agu, agu_oth),
                      (wob, attv, xb, mido, aob, bob, agub), wo_sem, lo_sem)
 
     def gu_copies(k, own):
@@ -859,7 +875,7 @@
     start(bd_copies)
     sel[...] = pick(sel.shape, share, rank, 2, 1)
     for k in range(2):
-        start(stage.wo_copies(k))
+        stage.wo_start(k)
         start(gu_copies(k, True))
         start(wd_copies(k))
     att_start(jnp.int32(1))
@@ -1023,7 +1039,7 @@
             hop.wait_send()
 
 
-def call_b(n, keep, scale, rank, share, x, gain, att, wo, wo_l, wo_r, wo_f, wo_x, wide, wide_f, wide_x, agu, agu_oth, wg, wg_o, wu, wu_o, wd, wd_o, lml, lml_o, h_first, x1_first, mg_first):
+def call_b(n, keep, scale, rank, share, x, gain, att, wo, wo_p, wo_f, wo_x, wide, wide_f, wide_x, agu, agu_oth, wg, wg_o, wu, wu_o, wd, wd_o, lml, lml_o, h_first, x1_first, mg_first):
     nseq, rows, model, ff = att.shape[0], x.shape[1], x.shape[2], wg.shape[1]
     hbm = pl.BlockSpec(memory_space=pl.ANY)
     vmem = pl.BlockSpec(memory_space=pltpu.VMEM)
@@ -1035,7 +1051,7 @@
     return pl.pallas_call(
         functools.partial(kernel_b, n, keep, scale, rank, share),
         out_shape=[jax.ShapeDtypeStruct(x.shape, BF16), jax.ShapeDtypeStruct((nseq - keep, *att.shape[1:]), BF16)],
-        in_specs=[hbm, vmem] + [hbm] * 22,
+        in_specs=[hbm, vmem] + [hbm] * 21,
         out_specs=[hbm] * 2,
         scratch_shapes=[
             pltpu.VMEM((PAIR, model, tile), BF16),
@@ -1072,7 +1088,7 @@
         compiler_params=pltpu.CompilerParams(collective_id=1, has_side_effects=True, vmem_limit_bytes=VMEM_LIMIT),
         cost_estimate=pl.CostEstimate(flops=flops, bytes_accessed=4 * x.size, transcendentals=0),
         name="out_mlp",
-    )(x, gain, att, wo, wo_l, wo_r, wo_f, wo_x, wide, wide_f, wide_x, agu, agu_oth, wg, wg_o, wu, wu_o, wd, wd_o, lml, lml_o, h_first, x1_first, mg_first)[0]
+    )(x, gain, att, wo, wo_p, wo_f, wo_x, wide, wide_f, wide_x, agu, agu_oth, wg, wg_o, wu, wu_o, wd, wd_o, lml, lml_o, h_first, x1_first, mg_first)[0]
 
 
 def solution(mesh):
@@ -1102,9 +1118,8 @@
 
         wo = w_o.reshape(own, model)
         ndev = n * CORES
-        upper = wo[:own // 2]
-        wo_l = lax.ppermute(upper, "tp", [(d, (d + CORES) % ndev) for d in range(ndev)])
-        wo_r = lax.ppermute(upper, "tp", [((d + CORES) % ndev, d) for d in range(ndev)])
+        turns = [(d, (d + CORES * (1 if d % CORES == 0 else -1)) % ndev) for d in range(ndev)]
+        wo_p = lax.ppermute(wo, "tp", turns)
         ar = take(turn(a_q), turn(a_k), turn(a_v), jnp.zeros((a_q.shape[0], share, model), BF16))
         agu = take(turn(a_gate), turn(a_up))
         bqkv = take(*[b.reshape(-1, rank, own) for b in (b_q, b_k, b_v)])
@@ -1113,8 +1128,8 @@
         flat = [jnp.transpose(w, (1, 2, 0)).reshape(own, model) for w in (w_q, w_k, w_v)]
         att, _, agu_oth, _, wide_f, wide_x, wo_f, wo_x, wg_o, wu_o, wd_o, lml_o, *head = call_a(
             n, keep, scale, group, dim, share, x_in, gain_attn.reshape(1, model), gain_mlp.reshape(1, model), *flat, ar, agu, bqkv, wide,
-            wo, wo_l, wo_r, w_gate, w_up, w_down, lml)
-        return call_b(n, keep, scale, rank, share, x_in, gain_mlp.reshape(1, model), att, wo, wo_l, wo_r, wo_f, wo_x, wide, wide_f, wide_x,
+            wo, wo_p, w_gate, w_up, w_down, lml)
+        return call_b(n, keep, scale, rank, share, x_in, gain_mlp.reshape(1, model), att, wo, wo_p, wo_f, wo_x, wide, wide_f, wide_x,
                       agu, agu_oth, w_gate, wg_o, w_up, wu_o, w_down, wd_o, lml, lml_o, *head)
 
     return jax.shard_map(local_layer, mesh=mesh, in_specs=in_specs, out_specs=act_spec, check_vma=False)

time: 805 us -> 808 us (level)
    pallas_call x1, Pallas kernels: 235 us -> 246 us  [call_a(): pl.pallas_call(functools.partial(kernel_a, n, lag, keep, scale, group, di...]
    unnamed x26 -> x20, local copies, waits for them, and re-layouts: 33.7 us -> 33.6 us
  transfers between devices with their start and end apart: 2 -> 1, of which waited for: 2 -> 1; matrix products, arithmetic and copies ran while one was open for 2% -> 2% of each run, Pallas kernels for 0% -> 0%
where the time goes in v3:
time: 808 us; the launch traced here: 807 us
  Pallas kernels  745 us (92%)
  local copies, waits for them, and re-layouts  47.6 us (6%)
    pallas_call x1, Pallas kernels, call_b(): pl.pallas_call(functools.partial(kernel_b, n, keep, scale, rank, share),...  499 us
    pallas_call x1, Pallas kernels, call_a(): pl.pallas_call(functools.partial(kernel_a, n, lag, keep, scale, group, di...  246 us
    unnamed x20, local copies, waits for them, and re-layouts  33.6 us
  transfers between devices with their start and end apart: 1, of which 1 were waited for; matrix products, arithmetic and copies ran while one was open for 2% of the time, Pallas kernels for 0%

profile of v3, /device:TPU:113, one launch (start us, length us, event | category | flops | bytes accessed | tf_op | source)
XLA Modules:
  0.0 807.4 jit_solution(18368659020593277349)
XLA Ops:
  0.0 3.7 collective-permute-start
  3.7 1.4 reshape.36
  5.2 1.4 reshape.37
  6.6 1.4 reshape.38
  8.1 0.3 copy.26
  8.4 0.4 reshape.39
  8.8 0.0 copy-start.1
  8.8 0.0 copy-start.2
  8.8 0.1 pad_maximum_fusion.1
  8.9 1.7 gather_fusion.2
  10.7 0.1 pad_maximum_fusion.2
  10.8 0.0 copy-start.6
  10.8 1.7 gather_fusion.3
  12.5 0.4 pad_maximum_fusion.3
  12.9 1.5 gather_fusion.1
  14.4 0.1 pad.14.clone
  14.5 0.8 maximum_maximum_fusion
  15.3 1.9 gather_fusion
  17.1 2.0 pad_maximum_fusion
  19.2 2.4 gather_fusion.4
  21.6 7.9 collective-permute-done.wo_p
  29.5 245.6 %qkv_attention.1 = (bf16[8,4,512,768]{3,2,1,0:T(8,128)(2,1)}, bf16[8,16,3072]{2,1,0:T(8,128)(2,1)}, bf16[8,8,3072]{2,1,0:T(8,128)(2,1)}, bf16[8,96,384]{2,1,0:T(...) custom-call(bf16[16,512,3072]{2,1,0:T(8,128)(2,1)} %x.3, ...), custom_call_target="tpu_custom_call" | custom-call | flops 60397977600 | bytes 75497472 | tf_op jit(solution)/shard_map/qkv_attention/pallas_call | solution.py:577
  275.1 499.0 %out_mlp.1 = (bf16[16,512,3072]{2,1,0:T(8,128)(2,1)}, bf16[3,4,512,768]{3,2,1,0:T(8,128)(2,1)}) custom-call(bf16[16,512,3072]{2,1,0:T(8,128)(2,1)} %x.3, f32[1,3072]{1,0:T(1,128)} %bitcast.36, bf16[8,4,512,768]{3,2,1,0:T(8,128)(2,1)} %get-tuple-element.19.att, bf16[384,3072]{1,0:T(8,128)(2,1)} %bitcast.33, bf16[384,3072]{1,0:T(8,128)(2,1)} %collective-permute-done.wo_p, ...), custom_call_target="tpu_custom_call" | custom-call | flops 231928233984 | bytes 100663296 | tf_op jit(solution)/shard_map/out_mlp/pallas_call | solution.py:1051
  774.1 33.3 %copy.28 = bf16[16,512,3072]{2,1,0:T(8,128)(2,1)} copy(bf16[16,512,3072]{2,1,0:T(8,128)(2,1)} %get-tuple-element.32) | data formatting | bytes 100663296
  (17 shorter events, 0.0 us)
Async XLA Ops:
  0.0 8.1 %copy-start = (bf16[16,4,96,32]{2,3,1,0:T(8,128)(2,1)S(1)}, bf16[16,4,96,32]{2,3,1,0:T(8,128)(2,1)}, u32[]{:S(2)}) copy-start(bf16[16,4,96,32]{2,3,1,0:T(8,128)(2,1)} %param.42) | copy-start | bytes 1179652
  0.0 8.7 %copy-start.8 = (s32[16]{0:T(128)S(1)}, s32[16]{0:T(128)}, u32[]{:S(2)}) copy-start(s32[16]{0:T(128)} %param.26) | copy-start | bytes 196
  0.0 29.5 %collective-permute-start = (bf16[384,3072]{1,0:T(8,128)(2,1)}, bf16[384,3072]{1,0:T(8,128)(2,1)}, u32[]{:S(2)}, u32[]{:S(2)}) collective-permute-start(bf16[384,3072]{1,0:T(8,128)(2,1)} %bitcast.31), channel_id=1, source_target_pairs={{0,2},{1,7},{2,4},{3,1},{4,6},{5,3},{6,0},{7,5},{8,10},{9,15},{10,... | collective-permute-start | bytes 7077896 | tf_op jit(solution)/shard_map/ppermute | solution.py:1122
  8.8 1.9 copy-start.1
  8.8 1.9 copy-start.2
  10.7 1.9 copy-start.3
  10.7 1.9 copy-start.4
  10.8 3.7 copy-start.5
  10.8 3.7 copy-start.6
  12.5 2.0 copy-start.7
